TPU v7x, 128 devices: a whole 4x4x4 slice. The times are simulated.
128 devices in a mesh: gz: 128 (over y, z, x, core).
Axes of the slice: x: 4, y: 4, z: 4, core: 2. Of those that a mesh axis runs over, the one named last changes fastest.
Arguments:
- marker_positions: float32 [16384, 3, 256], P('gz'), may hold values from 0 to 1
- marker_forces: float32 [16384, 3, 256], P('gz'), may hold values from -48 to 48
- dest_slab: int32 [16384, 1], P('gz'), may hold values from 0 to 127; in each aligned block of 128 rows (0 to 127, 128 to 255, ...) at most 2 rows name the same one
- base_cells: int32 [16384, 2], P('gz'), may hold values from 0 to 127
- fluid_source: float32 [512, 3, 128, 128], P('gz'), may hold values from -7 to 7
Outputs:
- velocity: float32 [512, 3, 128, 128], P('gz')
- marker_velocity: float32 [16384, 3, 256], P('gz')
Inputs may be any that keep to these rules, and one draw needn't show every extreme that they name: `dest_slab`: among the blocks of one device no slab is named more than 2 times.
All inputs are finite; a program needn't handle non-finite values.
Results may differ from a plain program's by a relative error of at most 0.00096.
Values may be sent and summed in bfloat16 or wider, within the bound.
No kernel may reach another device: no remote copies, remote signals or barrier semaphores. Data moves between devices by JAX's collectives and lax.ppermute only.
A program may use at most 256 MiB of HBM per device.

v0:
```python
import math

import jax
import jax.numpy as jnp
from jax import lax
from jax.sharding import Mesh
from jax.sharding import PartitionSpec as P

CZ = 4
BOX = 16
SWEEPS = 2
CSWEEPS = 6
GZ = ("gz_0", "gz_1", "gz_2", "gz_3")


screening = 1.0 / 64.0
relaxation = 2.0 / 3.0


def padded_2(array, sides, width):
    for axis, dim in sides:
        size, length = (lax.axis_size(axis), array.shape[dim])
        up = [(i, (i + 1) % size) for i in range(size)]
        down = [(j, i) for i, j in up]
        last = lax.slice_in_dim(array, length - width, length, axis=dim)
        initial = lax.slice_in_dim(array, 0, width, axis=dim)
        before = lax.ppermute(last, axis, up)
        after = lax.ppermute(initial, axis, down)
        array = jnp.concatenate([before, array, after], axis=dim)
    return array


def laid_out(pieces, dim):
    dims = list(pieces.shape[1:])
    dims[dim] *= pieces.shape[0]
    return jnp.moveaxis(pieces, 0, dim).reshape(dims)


def stacked_from(array, axes, order):
    pieces = array
    for k in order:
        pieces = lax.all_gather(pieces, axes[k])
    done = order[::-1]
    back = [done.index(k) for k in range(len(axes))]
    pieces = pieces.transpose(*back, *range(len(axes), pieces.ndim))
    return pieces.reshape(-1, *array.shape)


def gathered_by_axis(array, axes, order, dim):
    return laid_out(stacked_from(array, axes, order), dim)


def kernel_phi(offset):
    inside = jnp.abs(offset) < 2.0
    return jnp.where(inside, 0.25 * (1.0 + jnp.cos(0.5 * jnp.pi * offset)), 0.0 * offset)


def kernel_tables(positions):
    box_cells = jnp.arange(BOX, dtype=positions.dtype)
    slab_cells = jnp.arange(CZ, dtype=positions.dtype)
    across = 2.0 + (BOX - 5) * positions[:, 0, :]
    along_y = 2.0 + (BOX - 5) * positions[:, 1, :]
    height = (CZ - 1) * positions[:, 2, :]
    weight_x = kernel_phi(across[:, :, None] - box_cells)
    weight_y = kernel_phi(along_y[:, :, None] - box_cells)
    weight_z = kernel_phi(height[:, :, None] - slab_cells)
    plane_weight = (weight_x[:, :, :, None] * weight_y[:, :, None, :]).reshape(
        positions.shape[0], positions.shape[2], BOX * BOX
    )
    return (weight_z, plane_weight)


def build_boxes(positions, forces):
    weight_z, plane_weight = kernel_tables(positions)
    loaded = jnp.einsum("bmk,bcm->bkcm", weight_z, forces, precision=lax.Precision.HIGHEST)
    box_values = jnp.einsum("bkcm,bmq->bkcq", loaded, plane_weight, precision=lax.Precision.HIGHEST)
    return box_values.reshape(positions.shape[0], -1).astype(jnp.bfloat16)


def read_boxes(positions, box_velocity):
    weight_z, plane_weight = kernel_tables(positions)
    block_total = positions.shape[0]
    box_values = box_velocity.astype(jnp.float32).reshape(block_total, CZ, 3, BOX * BOX)
    spread = jnp.einsum("bkcq,bmq->bkcm", box_values, plane_weight, precision=lax.Precision.HIGHEST)
    return jnp.einsum("bmk,bkcm->bcm", weight_z, spread, precision=lax.Precision.HIGHEST)


def grouped(function, arrays):
    block_total = arrays[0].shape[0]
    group_rows = math.gcd(block_total, 32)
    stacked = tuple(
        (
            member.reshape((block_total // group_rows, group_rows) + member.shape[1:])
            for member in arrays
        )
    )
    result = lax.map(lambda pieces: function(*pieces), stacked)
    return result.reshape((block_total,) + result.shape[2:])


def selector(first_cell, grid_width):
    box_cells = (first_cell[:, None] + jnp.arange(BOX, dtype=jnp.int32)[None, :]) % grid_width
    grid_cells = jnp.arange(grid_width, dtype=jnp.int32)
    return (grid_cells[None, :, None] == box_cells[:, None, :]).astype(jnp.bfloat16)


def place_boxes(arrived, arrived_base, grid_width):
    slot_count = arrived.shape[0]
    group_rows = math.gcd(slot_count, 32)
    group_count = slot_count // group_rows

    def place(running, pieces):
        group_boxes, group_base = pieces
        box_values = group_boxes.reshape(group_rows, CZ, 3, BOX, BOX)
        select_x = selector(group_base[:, 0], grid_width)
        select_y = selector(group_base[:, 1], grid_width)
        along_x = jnp.einsum(
            "gxi,gzcij->gzcxj", select_x, box_values, preferred_element_type=jnp.float32
        ).astype(jnp.bfloat16)
        return (
            running
            + jnp.einsum("gzcxj,gyj->zcxy", along_x, select_y, preferred_element_type=jnp.float32),
            None,
        )

    start_grid = jnp.zeros((CZ, 3, grid_width, grid_width), jnp.float32)
    force_grid, unused = lax.scan(
        place,
        start_grid,
        (
            arrived.reshape(group_count, group_rows, -1),
            arrived_base.reshape(group_count, group_rows, 2),
        ),
    )
    return force_grid


def pick_boxes(velocity_low, arrived_base, grid_width):

    def pick(group_base):
        group_size = group_base.shape[0]
        select_x = selector(group_base[:, 0], grid_width)
        select_y = selector(group_base[:, 1], grid_width)
        along_y = jnp.einsum(
            "zcxy,gyj->gzcxj", velocity_low, select_y, preferred_element_type=jnp.float32
        ).astype(jnp.bfloat16)
        box_values = jnp.einsum(
            "gzcxj,gxi->gzcij", along_y, select_x, preferred_element_type=jnp.float32
        )
        return box_values.astype(jnp.bfloat16).reshape(group_size, -1)

    return grouped(pick, (arrived_base,))


def operate(solution, level_index, shared):
    if shared:
        padded = padded_2(solution, ((GZ, 0),), 1)
        upper_layer = padded[2:]
        lower_layer = padded[:-2]
    else:
        upper_layer = jnp.roll(solution, -1, 0)
        lower_layer = jnp.roll(solution, 1, 0)
    beside = upper_layer + lower_layer
    beside = beside + jnp.roll(solution, -1, 2) + jnp.roll(solution, 1, 2)
    beside = beside + jnp.roll(solution, -1, 3) + jnp.roll(solution, 1, 3)
    return screening * solution - 0.25**level_index * (beside - 6.0 * solution)


def relax_factor(level_index):
    return relaxation / (screening + 6.0 * 0.25**level_index)


def restrict(solution):
    shape_now = solution.shape
    folded = solution.reshape(
        shape_now[0] // 2, 2, shape_now[1], shape_now[2] // 2, 2, shape_now[3] // 2, 2
    )
    return jnp.mean(folded, axis=(1, 4, 6))


def prolong(solution):
    return jnp.repeat(jnp.repeat(jnp.repeat(solution, 2, 0), 2, 2), 2, 3)


def descend(source, level_index):
    factor = relax_factor(level_index)
    solution = factor * source
    solution = solution + factor * (source - operate(solution, level_index, True))
    return (solution, source - operate(solution, level_index, True))


def ascend(solution, source, level_index):
    factor = relax_factor(level_index)
    for sweep_turn in range(SWEEPS):
        solution = solution + factor * (source - operate(solution, level_index, True))
    return solution


def coarsest(source):
    factor = relax_factor(3)
    solution = factor * source
    for sweep_turn in range(CSWEEPS - 1):
        solution = solution + factor * (source - operate(solution, 3, False))
    leftover = source - operate(solution, 3, False)
    level_mean = jnp.mean(leftover, axis=(0, 2, 3), keepdims=True)
    return solution + level_mean / screening


def collect(layers_here):
    return gathered_by_axis(layers_here, GZ, (0, 1, 2, 3), 0)


def shards(marker_positions, marker_forces, dest_slab, base_cells, fluid_source):
    devices = lax.axis_size(GZ)
    grid_width = fluid_source.shape[2]
    held_blocks = marker_positions.shape[0]
    capacity = max(2, 2 * held_blocks // devices)
    slot_count = devices * capacity
    target = dest_slab[:, 0]
    dest_hits = (target[:, None] == jnp.arange(devices, dtype=jnp.int32)[None, :]).astype(jnp.int32)
    before = jnp.cumsum(dest_hits, axis=0) - dest_hits
    slot_order = jnp.sum(before * dest_hits, axis=1)
    slot_index = target * capacity + slot_order
    base_sent = jnp.zeros((slot_count, 2), jnp.int32).at[slot_index].set(base_cells)
    own_boxes = grouped(build_boxes, (marker_positions, marker_forces))
    box_sent = (
        jnp.zeros((slot_count, own_boxes.shape[1]), jnp.bfloat16).at[slot_index].set(own_boxes)
    )
    arrived, arrived_base = (
        lax.all_to_all(box_sent, GZ, split_axis=0, concat_axis=0, tiled=True),
        lax.all_to_all(base_sent, GZ, split_axis=0, concat_axis=0, tiled=True),
    )
    force_grid = place_boxes(arrived, arrived_base, grid_width)
    source = fluid_source + force_grid
    fine_sol, fine_res = descend(source, 0)
    middle_rhs = restrict(fine_res)
    middle_sol, middle_res = descend(middle_rhs, 1)
    third_rhs = restrict(middle_res)
    layers = third_rhs.shape[0]
    first_layer = lax.axis_index(GZ) * layers
    third_sol, third_res = descend(third_rhs, 2)
    whole_res = collect(third_res)
    coarse_sol = coarsest(restrict(whole_res))
    lifted = lax.dynamic_slice_in_dim(prolong(coarse_sol), first_layer, layers, 0)
    third_sol = ascend(third_sol + lifted, third_rhs, 2)
    middle_sol = ascend(middle_sol + prolong(third_sol), middle_rhs, 1)
    velocity = ascend(fine_sol + prolong(middle_sol), source, 0)
    velocity_low = velocity.astype(jnp.bfloat16)
    picked = pick_boxes(velocity_low, arrived_base, grid_width)
    returned = lax.all_to_all(picked, GZ, split_axis=0, concat_axis=0, tiled=True)
    marker_velocity = grouped(read_boxes, (marker_positions, returned[slot_index]))
    return (velocity, marker_velocity)


def solution(mesh):
    torus = Mesh(mesh.devices.reshape(4, 4, 4, 2), ("gz_0", "gz_1", "gz_2", "gz_3"))
    return jax.shard_map(
        shards,
        mesh=torus,
        in_specs=(
            P(GZ, None, None),
            P(GZ, None, None),
            P(GZ, None),
            P(GZ, None),
            P(GZ, None, None, None),
        ),
        out_specs=(P(GZ, None, None, None), P(GZ, None, None)),
        check_vma=False,
    )
```

profile of v0, /device:TPU:1, one launch (start us, length us, event | category | flops | bytes accessed | tf_op | source)
XLA Modules:
  0.0 686.6 jit_solution(589198339583883509)
XLA Ops:
  12.8 11.5 %all-to-all-start.1 = ((s32[128,2,2]{1,2,0:T(2,128)}), s32[128,2,2]{1,2,0:T(2,128)S(1)}, u32[]{:S(2)}, u32[]{:S(2)}) async-start(s32[128,2,2]{1,2,0:T(2,128)} %copy.96), calls=%async_computation.1 | async-start | bytes 262144 | tf_op jit(solution)/shard_map/all_to_all | solution.py:231
  25.7 53.5 %while.45 = (s32[]{:T(128)}, bf16[4,32,3072]{2,1,0:T(8,128)(2,1)S(1)}, f32[4,32,3,256]{3,2,1,0:T(4,128)S(1)}, f32[4,32,3,256]{3,1,2,0:T(8,128)S(1)}, s32[]{:T(128)}) while((s32[]{:T(128)}, bf16[4,32,3072]{2,1,0:T(8,128)(2,1)S(1)}, f32[4,32,3,256]{3,2,1,0:T(4,128)S(1)}, f32[4,32,3,256]{3,1,2,0:T(8,128)S(1)}, s32[]{:T(128)}) %tuple.236), condition=%wide.region_3.4_spmd, body=%wide.region_2.3_spmd.sunk | while | flops 306683904 | bytes 21299272 | solution.py:97
  31.5 7.1 %convolution_convert_fusion.5 = bf16[32,4,3,256]{3,1,2,0:T(4,128)(2,1)S(1)} fusion(f32[32,256,256,1]{1,2,3,0:T(8,128)S(1)} %bitcast.205, f32[32,256,4]{1,2,0:T(4,128)S(1)} %multiply_select_fusion.11, f32[32,256,3]{1,2,0:T(4,128)S(1)} %dynamic-slice_bitcast_fusion.11), kind=kOutput, calls=%fused_computation.4.clone.1 | convolution fusion | flops 302186496 | bytes 8814592 | tf_op jit(solution)/shard_map/while/body/eval_jaxpr/bkcm,bmq->bkcq/dot_general | solution.py:76
  44.8 7.1 %convolution_convert_fusion.5 = bf16[32,4,3,256]{3,1,2,0:T(4,128)(2,1)S(1)} fusion(f32[32,256,256,1]{1,2,3,0:T(8,128)S(1)} %bitcast.205, f32[32,256,4]{1,2,0:T(4,128)S(1)} %multiply_select_fusion.11, f32[32,256,3]{1,2,0:T(4,128)S(1)} %dynamic-slice_bitcast_fusion.11), kind=kOutput, calls=%fused_computation.4.clone.1 | convolution fusion | flops 302186496 | bytes 8814592 | tf_op jit(solution)/shard_map/while/body/eval_jaxpr/bkcm,bmq->bkcq/dot_general | solution.py:76
  58.1 7.1 %convolution_convert_fusion.5 = bf16[32,4,3,256]{3,1,2,0:T(4,128)(2,1)S(1)} fusion(f32[32,256,256,1]{1,2,3,0:T(8,128)S(1)} %bitcast.205, f32[32,256,4]{1,2,0:T(4,128)S(1)} %multiply_select_fusion.11, f32[32,256,3]{1,2,0:T(4,128)S(1)} %dynamic-slice_bitcast_fusion.11), kind=kOutput, calls=%fused_computation.4.clone.1 | convolution fusion | flops 302186496 | bytes 8814592 | tf_op jit(solution)/shard_map/while/body/eval_jaxpr/bkcm,bmq->bkcq/dot_general | solution.py:76
  71.5 7.1 %convolution_convert_fusion.5 = bf16[32,4,3,256]{3,1,2,0:T(4,128)(2,1)S(1)} fusion(f32[32,256,256,1]{1,2,3,0:T(8,128)S(1)} %bitcast.205, f32[32,256,4]{1,2,0:T(4,128)S(1)} %multiply_select_fusion.11, f32[32,256,3]{1,2,0:T(4,128)S(1)} %dynamic-slice_bitcast_fusion.11), kind=kOutput, calls=%fused_computation.4.clone.1 | convolution fusion | flops 302186496 | bytes 8814592 | tf_op jit(solution)/shard_map/while/body/eval_jaxpr/bkcm,bmq->bkcq/dot_general | solution.py:76
  83.7 9.8 %all-to-all-start = ((bf16[128,2,3072]{2,1,0:T(2,128)(2,1)}), bf16[128,2,3072]{2,1,0:T(2,128)(2,1)S(1)}, u32[]{:S(2)}, u32[]{:S(2)}) async-start(bf16[128,2,3072]{2,1,0:T(2,128)(2,1)} %all_to_all.20), calls=%async_computation | async-start | bytes 3145728 | tf_op jit(solution)/shard_map/all_to_all | solution.py:230
  94.8 23.5 %all-to-all-done = bf16[128,2,3072]{2,1,0:T(2,128)(2,1)S(1)} async-done(((bf16[128,2,3072]{2,1,0:T(2,128)(2,1)}), bf16[128,2,3072]{2,1,0:T(2,128)(2,1)S(1)}, u32[]{:S(2)}, u32[]{:S(2)}) %all-to-all-start) | async-done | bytes 1572896 | tf_op jit(solution)/shard_map/all_to_all | solution.py:230
  119.8 44.0 %while.48 = (s32[]{:T(128)}, f32[4,3,128,128]{3,2,1,0:T(8,128)S(1)}, bf16[8,32,3072]{2,1,0:T(8,128)(2,1)}, s32[8,32,2]{1,2,0:T(2,128)S(1)}, s32[]{:T(128)}, /*index=5*/s32[]{:T(128)}) while((s32[]{:T(128)}, f32[4,3,128,128]{3,2,1,0:T(8,128)S(1)}, bf16[8,32,3072]{2,1,0:T(8,128)(2,1)}, s32[8,32,2]{1,2,0:T(2,128)S(1)}, s32[]{:T(128)}, ...), condition=%wide.region_7.8_spmd.clone, body=%wide.region_6.7_spmd.clone.sunk | while | flops 227815424 | bytes 7677271 | solution.py:127
  172.5 7.1 %collective-permute-start.2 = (f32[1,3,128,128]{2,3,1,0:T(8,128)S(1)}, f32[1,3,128,128]{2,3,1,0:T(8,128)S(1)}, u32[]{:S(2)}, u32[]{:S(2)}) collective-permute-start(f32[1,3,128,128]{2,3,1,0:T(8,128)S(1)} %get-tuple-element.323), channel_id=1, source_target_pairs={{1,0},{2,1},{3,2},{4,3},{5,4},{6,5},{7,6},{8,7},{9,8},{10,9},{11,1... | collective-permute-start | bytes 589832 | tf_op jit(solution)/shard_map/ppermute | solution.py:28
  183.2 52.0 %reshape.356 = f32[2,2,3,64,2,64,2]{6,5,4,3,2,1,0:T(8,128)} reshape(f32[4,3,128,128]{3,2,1,0:T(8,128)S(1)} %copy.102) | data formatting | bytes 1572864 | tf_op jit(solution)/shard_map/reshape | solution.py:175
  235.2 17.9 %reduce_sum.65 = f32[2,3,64,64]{3,2,1,0:T(8,128)S(1)} reduce(f32[2,2,3,64,2,64,2]{6,5,4,3,2,1,0:T(8,128)} %reshape.356, f32[]{:T(128)} %constant.206.clone.1), dimensions={1,4,6}, to_apply=%region_8.9 | reduce | flops 172032 | bytes 884740 | tf_op jit(solution)/shard_map/reduce_sum | solution.py:178
  253.4 8.1 %collective-permute-start.4 = (f32[1,3,64,64]{3,2,1,0:T(8,128)S(1)}, f32[1,3,64,64]{3,2,1,0:T(8,128)S(1)}, u32[]{:S(2)}, u32[]{:S(2)}) collective-permute-start(f32[1,3,64,64]{3,2,1,0:T(8,128)S(1)} %get-tuple-element.445), channel_id=1, source_target_pairs={{1,0},{2,1},{3,2},{4,3},{5,4},{6,5},{7,6},{8,7},{9,8},{10,9},{11,1... | collective-permute-start | bytes 147464 | tf_op jit(solution)/shard_map/ppermute | solution.py:28
  263.6 8.0 %collective-permute-start.6 = (f32[1,3,64,64]{3,2,1,0:T(8,128)S(1)}, f32[1,3,64,64]{3,2,1,0:T(8,128)S(1)}, u32[]{:S(2)}, u32[]{:S(2)}) collective-permute-start(f32[1,3,64,64]{3,2,1,0:T(8,128)S(1)} %get-tuple-element.435), channel_id=1, source_target_pairs={{1,0},{2,1},{3,2},{4,3},{5,4},{6,5},{7,6},{8,7},{9,8},{10,9},{11,1... | collective-permute-start | bytes 147464 | tf_op jit(solution)/shard_map/ppermute | solution.py:28
  273.5 4.9 reduce_sum.67
  280.9 8.0 %collective-permute-start.8 = (f32[1,3,32,32]{3,2,1,0:T(8,128)S(1)}, f32[1,3,32,32]{3,2,1,0:T(8,128)S(1)}, u32[]{:S(2)}, u32[]{:S(2)}) collective-permute-start(f32[1,3,32,32]{3,2,1,0:T(8,128)S(1)} %multiply_bitcast_fusion), channel_id=1, source_target_pairs={{1,0},{2,1},{3,2},{4,3},{5,4},{6,5},{7,6},{8,7},{9,8},{10,9},{11,1... | collective-permute-start | bytes 36872 | tf_op jit(solution)/shard_map/ppermute | solution.py:28
  290.4 7.9 %collective-permute-start.10 = (f32[1,3,32,32]{3,2,1,0:T(8,128)S(1)}, f32[1,3,32,32]{3,2,1,0:T(8,128)S(1)}, u32[]{:S(2)}, u32[]{:S(2)}) collective-permute-start(f32[1,3,32,32]{3,2,1,0:T(8,128)S(1)} %fusion.208), channel_id=1, source_target_pairs={{1,0},{2,1},{3,2},{4,3},{5,4},{6,5},{7,6},{8,7},{9,8},{10,9},{11,1... | collective-permute-start | bytes 36872 | tf_op jit(solution)/shard_map/ppermute | solution.py:28
  299.6 9.2 %all-gather = f32[4,3,32,32]{3,2,1,0:T(8,128)S(1)} all-gather(f32[1,3,32,32]{3,2,1,0:T(8,128)S(1)} %fusion.215), channel_id=2, replica_groups=mesh['gz_0'=4,'gz_1'=4,'gz_2'=4,'gz_3'=2] {'gz_0'}, dimensions={0}, use_global_device_ids=true | all-gather | bytes 61440 | tf_op jit(solution)/shard_map/all_gather | solution.py:42
  308.9 10.7 %all-gather.1 = f32[16,3,32,32]{3,2,1,0:T(8,128)S(1)} all-gather(f32[4,3,32,32]{3,2,1,0:T(8,128)S(1)} %all-gather), channel_id=3, replica_groups=mesh['gz_0'=4,'gz_1'=4,'gz_2'=4,'gz_3'=2] {'gz_1'}, dimensions={0}, use_global_device_ids=true | all-gather | bytes 245760 | tf_op jit(solution)/shard_map/all_gather | solution.py:42
  319.6 23.8 %all-gather.2 = f32[16,4,1,3,32,32]{5,4,3,2,1,0:T(8,128)} all-gather(f32[4,4,1,3,32,32]{5,4,3,2,1,0:T(8,128)S(1)} %bitcast.218), channel_id=4, replica_groups=mesh['gz_0'=4,'gz_1'=4,'gz_2'=4,'gz_3'=2] {'gz_2'}, dimensions={0}, use_global_device_ids=true | all-gather | bytes 983040 | tf_op jit(solution)/shard_map/all_gather | solution.py:42
  343.4 27.4 %all-gather.6.cloned.1.call-done = f32[8,4,4,1,3,32,32]{6,5,4,3,2,1,0:T(8,128)} async-done(((f32[4,4,4,1,3,32,32]{6,5,4,3,2,1,0:T(8,128)}), f32[8,4,4,1,3,32,32]{6,5,4,3,2,1,0:T(8,128)}) %all-gather.6.cloned.1.call-update) | async-done | bytes 1572880 | tf_op jit(solution)/shard_map/all_gather | solution.py:42
  370.8 5.8 reduce.6
  376.7 21.7 %copy.105 = f32[4,4,4,3,32,32]{2,1,0,5,4,3:T(4,128)} copy(f32[4,4,4,3,32,32]{5,4,3,0,1,2:T(8,128)} %bitcast.209) | data formatting | bytes 1572864 | tf_op jit(solution)/shard_map/reduce_sum | solution.py:178
  398.3 30.1 %reduce_sum.71 = f32[64,3,16,2,16,2]{0,5,4,3,2,1:T(2,128)} reshape(f32[4,4,4,3,32,32]{2,1,0,5,4,3:T(4,128)} %copy.105) | data formatting | bytes 1572864 | tf_op jit(solution)/shard_map/reduce_sum | solution.py:178
  453.9 4.7 collective-permute-done.13
  458.9 8.3 %collective-permute-start.14 = (f32[1,3,32,32]{3,2,1,0:T(8,128)S(1)}, f32[1,3,32,32]{3,2,1,0:T(8,128)S(1)}, u32[]{:S(2)}, u32[]{:S(2)}) collective-permute-start(f32[1,3,32,32]{3,2,1,0:T(8,128)S(1)} %fusion.224), channel_id=1, source_target_pairs={{1,0},{2,1},{3,2},{4,3},{5,4},{6,5},{7,6},{8,7},{9,8},{10,9},{11,1... | collective-permute-start | bytes 36872 | tf_op jit(solution)/shard_map/ppermute | solution.py:28
  469.1 7.9 %collective-permute-start.16 = (f32[1,3,64,64]{3,2,1,0:T(8,128)S(1)}, f32[1,3,64,64]{3,2,1,0:T(8,128)S(1)}, u32[]{:S(2)}, u32[]{:S(2)}) collective-permute-start(f32[1,3,64,64]{3,2,1,0:T(8,128)S(1)} %get-tuple-element.425), channel_id=1, source_target_pairs={{1,0},{2,1},{3,2},{4,3},{5,4},{6,5},{7,6},{8,7},{9,8},{10,9},{11,1... | collective-permute-start | bytes 147464 | tf_op jit(solution)/shard_map/ppermute | solution.py:28
  479.2 8.0 %collective-permute-start.18 = (f32[1,3,64,64]{3,2,1,0:T(8,128)S(1)}, f32[1,3,64,64]{3,2,1,0:T(8,128)S(1)}, u32[]{:S(2)}, u32[]{:S(2)}) collective-permute-start(f32[1,3,64,64]{3,2,1,0:T(8,128)S(1)} %get-tuple-element.415), channel_id=1, source_target_pairs={{1,0},{2,1},{3,2},{4,3},{5,4},{6,5},{7,6},{8,7},{9,8},{10,9},{11,1... | collective-permute-start | bytes 147464 | tf_op jit(solution)/shard_map/ppermute | solution.py:28
  490.8 8.0 %collective-permute-start.20 = (f32[1,3,128,128]{2,3,1,0:T(8,128)S(1)}, f32[1,3,128,128]{2,3,1,0:T(8,128)S(1)}, u32[]{:S(2)}, u32[]{:S(2)}) collective-permute-start(f32[1,3,128,128]{2,3,1,0:T(8,128)S(1)} %get-tuple-element.313), channel_id=1, source_target_pairs={{1,0},{2,1},{3,2},{4,3},{5,4},{6,5},{7,6},{8,7},{9,8},{10,9},{11,1... | collective-permute-start | bytes 589832 | tf_op jit(solution)/shard_map/ppermute | solution.py:28
  502.9 8.1 %collective-permute-start.22 = (f32[1,3,128,128]{2,3,1,0:T(8,128)S(1)}, f32[1,3,128,128]{2,3,1,0:T(8,128)S(1)}, u32[]{:S(2)}, u32[]{:S(2)}) collective-permute-start(f32[1,3,128,128]{2,3,1,0:T(8,128)S(1)} %get-tuple-element.295), channel_id=1, source_target_pairs={{1,0},{2,1},{3,2},{4,3},{5,4},{6,5},{7,6},{8,7},{9,8},{10,9},{11,1... | collective-permute-start | bytes 589832 | tf_op jit(solution)/shard_map/ppermute | solution.py:28
  515.4 55.4 %while.46 = (s32[]{:T(128)}, bf16[8,32,3072]{2,1,0:T(8,128)(2,1)}, s32[8,32,2]{1,2,0:T(2,128)S(1)}, bf16[4,3,128,128]{3,2,1,0:T(8,128)(2,1)S(1)}, s32[]{:T(128)}) while((s32[]{:T(128)}, bf16[8,32,3072]{2,1,0:T(8,128)(2,1)}, s32[8,32,2]{1,2,0:T(2,128)S(1)}, bf16[4,3,128,128]{3,2,1,0:T(8,128)(2,1)S(1)}, s32[]{:T(128)}) %tuple.237), condition=%wide.region_15.16_spmd, body=%wide.region_14.15_spmd.sunk | while | flops 227520512 | bytes 1779521 | solution.py:97
  515.7 4.2 fusion.359
  522.6 4.2 fusion.359
  529.5 4.2 fusion.359
  557.0 4.2 fusion.359
  563.9 4.2 fusion.359
  570.7 4.5 all_to_all.24
  575.2 11.6 %all-to-all-start.2 = ((bf16[128,2,3072]{2,1,0:T(2,128)(2,1)}), bf16[128,2,3072]{2,1,0:T(2,128)(2,1)S(1)}, u32[]{:S(2)}, u32[]{:S(2)}) async-start(bf16[128,2,3072]{2,1,0:T(2,128)(2,1)} %all_to_all.24), calls=%async_computation.2 | async-start | bytes 3145728 | tf_op jit(solution)/shard_map/all_to_all | solution.py:250
  587.9 23.8 %all-to-all-done.2 = bf16[128,2,3072]{2,1,0:T(2,128)(2,1)S(1)} async-done(((bf16[128,2,3072]{2,1,0:T(2,128)(2,1)}), bf16[128,2,3072]{2,1,0:T(2,128)(2,1)S(1)}, u32[]{:S(2)}, u32[]{:S(2)}) %all-to-all-start.2) | async-done | bytes 1572896 | tf_op jit(solution)/shard_map/all_to_all | solution.py:250
  613.4 65.4 %while.47 = (s32[]{:T(128)}, f32[4,32,3,256]{3,1,0,2:T(8,128)S(1)}, bf16[4,32,3072]{2,1,0:T(8,128)(2,1)S(1)}, f32[4,32,3,256]{3,1,2,0:T(8,128)}, s32[]{:T(128)}) while((s32[]{:T(128)}, f32[4,32,3,256]{3,1,0,2:T(8,128)S(1)}, bf16[4,32,3072]{2,1,0:T(8,128)(2,1)S(1)}, f32[4,32,3,256]{3,1,2,0:T(8,128)}, s32[]{:T(128)}) %tuple.238), condition=%wide.region_17.18_spmd, body=%wide.region_16.17_spmd.sunk | while | flops 306659328 | bytes 21200968 | solution.py:97
  617.9 4.6 broadcast_multiply_fusion.9
  623.4 6.3 fusion.363
  634.3 4.6 broadcast_multiply_fusion.9
  639.8 6.3 fusion.363
  650.6 4.6 broadcast_multiply_fusion.9
  656.1 6.3 fusion.363
  667.0 4.6 broadcast_multiply_fusion.9
  672.5 6.3 fusion.363
  (408 shorter events, 204.5 us)
Async XLA Ops:
  7.2 18.2 %copy-start.4 = (f32[128,3,256]{2,0,1:T(8,128)S(1)}, f32[128,3,256]{2,0,1:T(8,128)}, u32[]{:S(2)}) copy-start(f32[128,3,256]{2,0,1:T(8,128)} %param.14) | copy-start | bytes 1179652
  12.8 70.8 %all-to-all-start.1 = ((s32[128,2,2]{1,2,0:T(2,128)}), s32[128,2,2]{1,2,0:T(2,128)S(1)}, u32[]{:S(2)}, u32[]{:S(2)}) async-start(s32[128,2,2]{1,2,0:T(2,128)} %copy.96), calls=%async_computation.1 | async-start | bytes 262144 | tf_op jit(solution)/shard_map/all_to_all | solution.py:231
  79.2 0.7 copy-start
  83.7 9.8 %copy-start.3 = (f32[4,3,128,128]{3,2,1,0:T(8,128)S(1)}, f32[4,3,128,128]{3,2,1,0:T(8,128)}, u32[]{:S(2)}) copy-start(f32[4,3,128,128]{3,2,1,0:T(8,128)} %param.17) | copy-start | bytes 2359300
  83.7 34.6 %all-to-all-start = ((bf16[128,2,3072]{2,1,0:T(2,128)(2,1)}), bf16[128,2,3072]{2,1,0:T(2,128)(2,1)S(1)}, u32[]{:S(2)}, u32[]{:S(2)}) async-start(bf16[128,2,3072]{2,1,0:T(2,128)(2,1)} %all_to_all.20), calls=%async_computation | async-start | bytes 3145728 | tf_op jit(solution)/shard_map/all_to_all | solution.py:230
  93.4 277.4 %all-gather.6.cloned.1.call-start = ((), (), s32[]{:S(2)}) async-start(), calls=%async_computation.3 | async-start | bytes 9437184 | tf_op jit(solution)/shard_map/all_gather | solution.py:42
  163.8 1.1 copy-start.2
  165.8 5.2 collective-permute-start
  166.9 4.1 collective-permute-start.1
  172.5 8.2 %collective-permute-start.2 = (f32[1,3,128,128]{2,3,1,0:T(8,128)S(1)}, f32[1,3,128,128]{2,3,1,0:T(8,128)S(1)}, u32[]{:S(2)}, u32[]{:S(2)}) collective-permute-start(f32[1,3,128,128]{2,3,1,0:T(8,128)S(1)} %get-tuple-element.323), channel_id=1, source_target_pairs={{1,0},{2,1},{3,2},{4,3},{5,4},{6,5},{7,6},{8,7},{9,8},{10,9},{11,1... | collective-permute-start | bytes 589832 | tf_op jit(solution)/shard_map/ppermute | solution.py:28
  179.6 2.6 collective-permute-start.3
  253.4 9.0 %collective-permute-start.4 = (f32[1,3,64,64]{3,2,1,0:T(8,128)S(1)}, f32[1,3,64,64]{3,2,1,0:T(8,128)S(1)}, u32[]{:S(2)}, u32[]{:S(2)}) collective-permute-start(f32[1,3,64,64]{3,2,1,0:T(8,128)S(1)} %get-tuple-element.445), channel_id=1, source_target_pairs={{1,0},{2,1},{3,2},{4,3},{5,4},{6,5},{7,6},{8,7},{9,8},{10,9},{11,1... | collective-permute-start | bytes 147464 | tf_op jit(solution)/shard_map/ppermute | solution.py:28
  261.4 1.6 collective-permute-start.5
  263.6 8.9 %collective-permute-start.6 = (f32[1,3,64,64]{3,2,1,0:T(8,128)S(1)}, f32[1,3,64,64]{3,2,1,0:T(8,128)S(1)}, u32[]{:S(2)}, u32[]{:S(2)}) collective-permute-start(f32[1,3,64,64]{3,2,1,0:T(8,128)S(1)} %get-tuple-element.435), channel_id=1, source_target_pairs={{1,0},{2,1},{3,2},{4,3},{5,4},{6,5},{7,6},{8,7},{9,8},{10,9},{11,1... | collective-permute-start | bytes 147464 | tf_op jit(solution)/shard_map/ppermute | solution.py:28
  271.6 1.6 collective-permute-start.7
  280.9 8.9 %collective-permute-start.8 = (f32[1,3,32,32]{3,2,1,0:T(8,128)S(1)}, f32[1,3,32,32]{3,2,1,0:T(8,128)S(1)}, u32[]{:S(2)}, u32[]{:S(2)}) collective-permute-start(f32[1,3,32,32]{3,2,1,0:T(8,128)S(1)} %multiply_bitcast_fusion), channel_id=1, source_target_pairs={{1,0},{2,1},{3,2},{4,3},{5,4},{6,5},{7,6},{8,7},{9,8},{10,9},{11,1... | collective-permute-start | bytes 36872 | tf_op jit(solution)/shard_map/ppermute | solution.py:28
  288.9 1.2 collective-permute-start.9
  290.4 8.7 %collective-permute-start.10 = (f32[1,3,32,32]{3,2,1,0:T(8,128)S(1)}, f32[1,3,32,32]{3,2,1,0:T(8,128)S(1)}, u32[]{:S(2)}, u32[]{:S(2)}) collective-permute-start(f32[1,3,32,32]{3,2,1,0:T(8,128)S(1)} %fusion.208), channel_id=1, source_target_pairs={{1,0},{2,1},{3,2},{4,3},{5,4},{6,5},{7,6},{8,7},{9,8},{10,9},{11,1... | collective-permute-start | bytes 36872 | tf_op jit(solution)/shard_map/ppermute | solution.py:28
  298.3 1.2 collective-permute-start.11
  450.4 3.6 collective-permute-start.12
  450.6 8.0 %collective-permute-start.13 = (f32[1,3,32,32]{3,2,1,0:T(8,128)S(1)}, f32[1,3,32,32]{3,2,1,0:T(8,128)S(1)}, u32[]{:S(2)}, u32[]{:S(2)}) collective-permute-start(f32[1,3,32,32]{3,2,1,0:T(8,128)S(1)} %add.665), channel_id=1, source_target_pairs={{0,1},{1,2},{2,3},{3,4},{4,5},{5,6},{6,7},{7,8},{8,9},{9,10},{10,1... | collective-permute-start | bytes 36872 | tf_op jit(solution)/shard_map/ppermute | solution.py:27
  458.9 9.2 %collective-permute-start.14 = (f32[1,3,32,32]{3,2,1,0:T(8,128)S(1)}, f32[1,3,32,32]{3,2,1,0:T(8,128)S(1)}, u32[]{:S(2)}, u32[]{:S(2)}) collective-permute-start(f32[1,3,32,32]{3,2,1,0:T(8,128)S(1)} %fusion.224), channel_id=1, source_target_pairs={{1,0},{2,1},{3,2},{4,3},{5,4},{6,5},{7,6},{8,7},{9,8},{10,9},{11,1... | collective-permute-start | bytes 36872 | tf_op jit(solution)/shard_map/ppermute | solution.py:28
  467.2 1.2 collective-permute-start.15
  469.1 8.8 %collective-permute-start.16 = (f32[1,3,64,64]{3,2,1,0:T(8,128)S(1)}, f32[1,3,64,64]{3,2,1,0:T(8,128)S(1)}, u32[]{:S(2)}, u32[]{:S(2)}) collective-permute-start(f32[1,3,64,64]{3,2,1,0:T(8,128)S(1)} %get-tuple-element.425), channel_id=1, source_target_pairs={{1,0},{2,1},{3,2},{4,3},{5,4},{6,5},{7,6},{8,7},{9,8},{10,9},{11,1... | collective-permute-start | bytes 147464 | tf_op jit(solution)/shard_map/ppermute | solution.py:28
  477.0 1.6 collective-permute-start.17
  479.2 8.9 %collective-permute-start.18 = (f32[1,3,64,64]{3,2,1,0:T(8,128)S(1)}, f32[1,3,64,64]{3,2,1,0:T(8,128)S(1)}, u32[]{:S(2)}, u32[]{:S(2)}) collective-permute-start(f32[1,3,64,64]{3,2,1,0:T(8,128)S(1)} %get-tuple-element.415), channel_id=1, source_target_pairs={{1,0},{2,1},{3,2},{4,3},{5,4},{6,5},{7,6},{8,7},{9,8},{10,9},{11,1... | collective-permute-start | bytes 147464 | tf_op jit(solution)/shard_map/ppermute | solution.py:28
  487.2 1.6 collective-permute-start.19
  490.8 9.1 %collective-permute-start.20 = (f32[1,3,128,128]{2,3,1,0:T(8,128)S(1)}, f32[1,3,128,128]{2,3,1,0:T(8,128)S(1)}, u32[]{:S(2)}, u32[]{:S(2)}) collective-permute-start(f32[1,3,128,128]{2,3,1,0:T(8,128)S(1)} %get-tuple-element.313), channel_id=1, source_target_pairs={{1,0},{2,1},{3,2},{4,3},{5,4},{6,5},{7,6},{8,7},{9,8},{10,9},{11,1... | collective-permute-start | bytes 589832 | tf_op jit(solution)/shard_map/ppermute | solution.py:28
  498.8 2.6 collective-permute-start.21
  502.9 9.1 %collective-permute-start.22 = (f32[1,3,128,128]{2,3,1,0:T(8,128)S(1)}, f32[1,3,128,128]{2,3,1,0:T(8,128)S(1)}, u32[]{:S(2)}, u32[]{:S(2)}) collective-permute-start(f32[1,3,128,128]{2,3,1,0:T(8,128)S(1)} %get-tuple-element.295), channel_id=1, source_target_pairs={{1,0},{2,1},{3,2},{4,3},{5,4},{6,5},{7,6},{8,7},{9,8},{10,9},{11,1... | collective-permute-start | bytes 589832 | tf_op jit(solution)/shard_map/ppermute | solution.py:28
  510.9 2.6 collective-permute-start.23
  575.2 11.6 %copy-start.1 = (f32[4,3,128,128]{2,3,1,0:T(8,128)S(1)}, f32[4,3,128,128]{2,3,1,0:T(8,128)}, u32[]{:S(2)}) copy-start(f32[4,3,128,128]{2,3,1,0:T(8,128)} %get-tuple-element.274) | copy-start | bytes 2359300
  575.2 36.5 %all-to-all-start.2 = ((bf16[128,2,3072]{2,1,0:T(2,128)(2,1)}), bf16[128,2,3072]{2,1,0:T(2,128)(2,1)S(1)}, u32[]{:S(2)}, u32[]{:S(2)}) async-start(bf16[128,2,3072]{2,1,0:T(2,128)(2,1)} %all_to_all.24), calls=%async_computation.2 | async-start | bytes 3145728 | tf_op jit(solution)/shard_map/all_to_all | solution.py:250
  612.4 1.1 copy-start.5
  678.9 0.7 copy-start.6
Sparse Core Ops, SparseCore 0:
  343.5 27.2 all-gather.5
where the time goes:
time: 698 us; the launch traced here: 687 us
  local copies, waits for them, and re-layouts  209 us (30%)
  starting transfers between devices  116 us (17%)
  waiting for transfers between devices  102 us (15%)
  other arithmetic  101 us (14%)
  matrix products  98.1 us (14%)
  blocking collectives  43.7 us (6%)
  between operations  15.2 us (2%)
    ppermute x12, starting transfers between devices, padded_2(): after = lax.ppermute(initial, axis, down)  80.5 us
    reduce_sum x3, local copies, waits for them, and re-layouts, restrict(): return jnp.mean(folded, axis=(1, 4, 6))  56.7 us
    reshape x1, local copies, waits for them, and re-layouts, restrict(): solution.reshape(shape_now[0] // 2, 2, shape_now[1], shape_now[2] // 2, 2...  52 us
    all_gather x3, blocking collectives, stacked_from(): pieces = lax.all_gather(pieces, axes[k])  43.7 us
    select_n x16, other arithmetic, kernel_phi(): jnp.where(inside, 0.25 * (1.0 + jnp.cos(0.5 * jnp.pi * offset)), 0.0 * of...  34 us
    dot_general x8, matrix products, pick(): jnp.einsum('gzcxj,gxi->gzcij', along_y, select_x, preferred_element_type=...  33.9 us
    reduce_sum x5, other arithmetic, restrict(): return jnp.mean(folded, axis=(1, 4, 6))  29 us
    dot_general x4, matrix products, build_boxes(): jnp.einsum('bkcm,bmq->bkcq', loaded, plane_weight, precision=lax.Precisio...  28.6 us
  transfers between devices with their start and end apart: 28, of which 26 were waited for; matrix products, arithmetic and copies ran while one was open for 9% of the time, Pallas kernels for 0%

commit v1 on v0

v1 whole, which is shorter than its diff:
```python
import jax
import jax.numpy as jnp
from jax import lax
from jax.experimental import pallas as pl
from jax.experimental.pallas import tpu as pltpu
from jax.sharding import PartitionSpec as P

AX = "gz"
BOX = 16
CZ = 4
ROWS = 24
SCREEN = 1.0 / 64.0
RELAX = 2.0 / 3.0
INTERPRET = False
F32 = jnp.float32
BF16 = jnp.bfloat16
HIGH = lax.Precision.HIGHEST


def level(index):
    q = 0.25**index
    return q, SCREEN + 6.0 * q, RELAX / (SCREEN + 6.0 * q)


def call(body, out_shape, in_specs=None, scratch=(), name=None, out_specs=None):
    options = {}
    if in_specs is not None:
        options["in_specs"] = in_specs
    if out_specs is not None:
        options["out_specs"] = out_specs
    return pl.pallas_call(
        body,
        out_shape=out_shape,
        scratch_shapes=list(scratch),
        name=name,
        interpret=INTERPRET,
        **options,
    )


VMEM = pl.BlockSpec(memory_space=pltpu.VMEM)
SMEM = pl.BlockSpec(memory_space=pltpu.SMEM)


def iota(shape, dim):
    return lax.broadcasted_iota(jnp.int32, shape, dim)


COS = (
    0.99999999999999999,
    -0.30842513753404244,
    0.015854344243815498,
    -0.00032599188692738954,
    3.5908604459003885e-06,
    -2.4611369504941976e-08,
    1.1500234922e-10,
)


def phi(offset):
    square = jnp.minimum(offset * offset, 4.0)
    value = jnp.full_like(square, COS[-1])
    for coefficient in COS[-2::-1]:
        value = value * square + coefficient
    value = 0.5 * (value * value)
    return jnp.where(square < 4.0, value, 0.0)


def split(value):
    high = value.astype(BF16)
    return high, (value - high.astype(F32)).astype(BF16)


def box_weights(pos_ref, block):
    cells = iota((BOX, 256), 0).astype(F32)
    levels = iota((8, 256), 0).astype(F32)
    row = pl.ds(block, 1)
    along_x = 2.0 + (BOX - 5) * pos_ref[0, row, :]
    along_y = 2.0 + (BOX - 5) * pos_ref[1, row, :]
    height = (CZ - 1) * pos_ref[2, row, :]
    return phi(along_x - cells), phi(along_y - cells), phi(height - levels)


def build_kernel(dest_ref, base_ref, pos_ref, frc_ref, out_ref, stage_ref, count_ref):
    slots = out_ref.shape[0]
    blocks = pos_ref.shape[1]

    def clear(t, carry):
        count_ref[t] = 0
        stage_ref[t] = jnp.zeros((2 * ROWS, 128), F32)
        return carry

    lax.fori_loop(0, slots, clear, 0)
    lane = iota((8, 128), 1)
    sub = iota((8, 128), 0)

    def one(block, carry):
        weight_x, weight_y, weight_z = box_weights(pos_ref, block)
        parts = []
        loaded = [weight_z * frc_ref[c, pl.ds(block, 1), :] for c in range(3)]
        for k in range(CZ):
            for c in range(3):
                parts.append(loaded[c][k : k + 1, :] * weight_x)
        whole = jnp.concatenate(parts, axis=0)
        high, low = split(whole)
        right = jnp.concatenate(split(weight_y), axis=0)
        dims = (((1,), (1,)), ((), ()))
        first = lax.dot_general(high, right, dims, preferred_element_type=F32)
        second = lax.dot_general(low, right[:BOX], dims, preferred_element_type=F32)
        box = first[:, :BOX] + first[:, BOX:] + second
        target = dest_ref[0, block]
        order = count_ref[target]
        count_ref[target] = order + 1
        base_x = base_ref[0, block].astype(F32) + 1.0
        base_y = base_ref[1, block].astype(F32)
        for q in range(3):
            packed = jnp.concatenate(
                [box[(8 * q + g) * 8 : (8 * q + g + 1) * 8] for g in range(8)], axis=1
            )
            if q == 0:
                top = sub == 0
                packed = jnp.where(top & (lane == 0), base_x, packed)
                packed = jnp.where(top & (lane == BOX), base_y, packed)
            stage_ref[target, pl.ds(pl.multiple_of(order * ROWS + 8 * q, 8), 8), :] = packed
        return carry

    lax.fori_loop(0, blocks, one, 0, unroll=2)

    def finish(t, carry):
        out_ref[t] = stage_ref[t].astype(BF16)
        return carry

    lax.fori_loop(0, slots, finish, 0, unroll=4)


def build(dest, base, positions, forces, slots):
    return call(
        build_kernel,
        jax.ShapeDtypeStruct((slots, 2 * ROWS, 128), BF16),
        [SMEM, SMEM, VMEM, VMEM],
        [pltpu.VMEM((slots, 2 * ROWS, 128), F32), pltpu.SMEM((slots,), jnp.int32)],
        "build",
    )(dest, base, positions, forces)


def place_kernel(meta_ref, pay_ref, fluid_ref, src_ref, bottom_ref, top_ref, grid_ref):
    slots = pay_ref.shape[0]
    lane = iota((8, 128), 1)
    sub = iota((8, 128), 0)
    for z in range(CZ):
        for c in range(3):
            grid_ref[3 * z + c, 0:128, :] = fluid_ref[z, c]
            grid_ref[3 * z + c, 128:144, :] = jnp.zeros((16, 128), F32)

    def add(tile, base_x, base_y):
        shift = base_x & 7
        row = pl.multiple_of(base_x - shift, 8)
        window = (lane - base_y) & 127
        inside = (window >= 1) & (window <= BOX - 2)
        late = inside & (sub >= shift)
        early = inside & (sub < shift)
        rolled = [pltpu.roll(tile[8 * q : 8 * q + 8], shift, 0) for q in range(3)]
        for kc in range(12):
            v = 2 * kc
            first = pltpu.roll(rolled[v // 8], (base_y - BOX * (v % 8)) & 127, 1)
            second = pltpu.roll(rolled[v // 8], (base_y - BOX * (v % 8 + 1)) & 127, 1)
            grid_ref[kc, pl.ds(row, 8), :] += jnp.where(late, first, 0.0)
            grid_ref[kc, pl.ds(row + 8, 8), :] += jnp.where(
                early, first, jnp.where(late, second, 0.0)
            )
            grid_ref[kc, pl.ds(row + 16, 8), :] += jnp.where(early, second, 0.0)

    def source_of(d, carry):
        for order in range(2):

            @pl.when(meta_ref[4 * d + 2 * order] > 0)
            def _():
                tile = pay_ref[d].astype(F32)
                add(
                    tile[order * ROWS : (order + 1) * ROWS],
                    meta_ref[4 * d + 2 * order] - 1,
                    meta_ref[4 * d + 2 * order + 1],
                )

        return carry

    lax.fori_loop(0, slots, source_of, 0)
    for z in range(CZ):
        for c in range(3):
            kc = 3 * z + c
            grid_ref[kc, 0:16, :] += grid_ref[kc, 128:144, :]
            value = grid_ref[kc, 0:128, :]
            src_ref[z, c] = value
            if z < 3:
                bottom_ref[z, c] = value
            if z > 0:
                top_ref[z - 1, c] = value


def place(meta, payload, fluid):
    width = fluid.shape[2]
    return call(
        place_kernel,
        (
            jax.ShapeDtypeStruct(fluid.shape, F32),
            jax.ShapeDtypeStruct((3, 3, width, width), F32),
            jax.ShapeDtypeStruct((3, 3, width, width), F32),
        ),
        [SMEM, VMEM, VMEM],
        [pltpu.VMEM((12, 144, 128), F32)],
        "place",
    )(meta, payload, fluid)


def flat_ring(x):
    rows = x.shape[-2]
    ax = x.ndim - 2
    return (
        pltpu.roll(x, 1, ax)
        + pltpu.roll(x, rows - 1, ax)
        + (pltpu.roll(x, 1, ax + 1) + pltpu.roll(x, 127, ax + 1))
    )


def group_ring(x):
    rows = x.shape[-2]
    ax = x.ndim - 2
    lane = iota(x.shape, ax + 1) & 31
    before = jnp.where(lane == 0, pltpu.roll(x, 97, ax + 1), pltpu.roll(x, 1, ax + 1))
    after = jnp.where(lane == 31, pltpu.roll(x, 31, ax + 1), pltpu.roll(x, 127, ax + 1))
    return pltpu.roll(x, 1, ax) + pltpu.roll(x, rows - 1, ax) + (before + after)


def start_of(b, below, above, ring, index):
    q, _, w = level(index)
    return w * ((4.0 / 3.0) * b + (w * q) * (ring(b) + (below + above)))


def left_of(b, u, below, above, ring, index):
    q, diag, _ = level(index)
    return b - diag * u + q * (ring(u) + (below + above))


def sweep_of(b, u, below, above, ring, index):
    q, _, w = level(index)
    return (1.0 - RELAX) * u + (w * b + (w * q) * (ring(u) + (below + above)))


def dot(left, right):
    return lax.dot_general(
        left, right, (((1,), (0,)), ((), ())), precision=HIGH, preferred_element_type=F32
    )


def lanes(test):
    return test(iota((128, 128), 0), iota((128, 128), 1))


def fine_kernel(low_ref, own_ref, high_ref, out_ref, u_ref, sum_ref):
    def b_at(z, c):
        if z < 0:
            return low_ref[z + 3, c]
        return own_ref[z, c] if z < CZ else high_ref[z - CZ, c]

    pool = [
        jnp.where(
            lanes(lambda r, l: (r // 2 == (l & 63)) & (l // 64 == half)), 0.125, 0.0
        )
        for half in range(2)
    ]

    def component(c, carry):
        for z in range(-1, CZ + 1):
            u_ref[z + 1] = start_of(b_at(z, c), b_at(z - 1, c), b_at(z + 1, c), flat_ring, 0)
        total = None
        for half in range(2):
            for z in (2 * half, 2 * half + 1):
                value = left_of(
                    own_ref[z, c], u_ref[z + 1], u_ref[z], u_ref[z + 2], flat_ring, 0
                )
                sum_ref[...] = value if z == 2 * half else sum_ref[...] + value
            rows = sum_ref[pl.ds(0, 64, 2), :] + sum_ref[pl.ds(1, 64, 2), :]
            part = dot(rows, pool[half])
            total = part if total is None else total + part
        out_ref[c] = total
        return carry

    lax.fori_loop(0, 3, component, 0)


def fine_down(low, own, high):
    return call(
        fine_kernel,
        jax.ShapeDtypeStruct((3, 64, 128), F32),
        None,
        [pltpu.VMEM((CZ + 2, 128, 128), F32), pltpu.VMEM((128, 128), F32)],
        "fine_down",
    )(low, own, high)


def both_layers(tile):
    lane = iota(tile.shape, tile.ndim - 1)
    turned = pltpu.roll(tile, 64, tile.ndim - 1)
    return jnp.where(lane < 64, tile, turned), jnp.where(lane < 64, turned, tile)


def pack_coarse(value):
    last = value[24:32]
    lane = iota((8, 128), 1)
    return [
        jnp.where(lane < 96, value[8 * c : 8 * c + 8], pltpu.roll(last, 96 - 32 * c, 1))
        for c in range(3)
    ]


def unpack_coarse(tile):
    lane = iota((8, 128), 1)
    last = jnp.zeros((8, 128), F32)
    rows = []
    for c in range(3):
        piece = tile[8 * c : 8 * c + 8]
        turned = pltpu.roll(piece, (32 * c - 96) % 128, 1)
        last = jnp.where(lane // 32 == c, turned, last)
        rows.append(jnp.where(lane < 96, piece, 0.0))
    return jnp.concatenate(rows + [last], axis=0)


def middle_kernel(low_ref, own_ref, high_ref, out_ref, sum_ref):
    total = None
    for c in range(3):
        b = []
        for ref in (low_ref, own_ref, high_ref):
            b.extend(both_layers(ref[c]))
        u = [start_of(b[i], b[i - 1], b[i + 1], flat_ring, 1) for i in range(1, 5)]
        left = [left_of(b[i + 1], u[i], u[i - 1], u[i + 1], flat_ring, 1) for i in (1, 2)]
        sum_ref[...] = left[0] + left[1]
        rows = sum_ref[pl.ds(0, 32, 2), :] + sum_ref[pl.ds(1, 32, 2), :]
        pool = jnp.where(
            lanes(lambda r, l: (r // 2 == (l & 31)) & (l // 32 == c) & (r < 64)), 0.125, 0.0
        )
        part = dot(rows, pool)
        total = part if total is None else total + part
    packed = jnp.concatenate(pack_coarse(total), axis=0)

    def copy(d, carry):
        out_ref[d] = packed
        return carry

    lax.fori_loop(0, out_ref.shape[0], copy, 0, unroll=8)


def middle_down(low, own, high, slots):
    return call(
        middle_kernel,
        jax.ShapeDtypeStruct((slots, 24, 128), F32),
        None,
        [pltpu.VMEM((64, 128), F32)],
        "middle_down",
    )(low, own, high)


def inner(x):
    return x[1:-1]


def coarse_part(me, g2_ref, pool_ref, final_ref):
    slots = g2_ref.shape[0]
    parity = me % 2
    first = me - parity - 16 + 16 * slots
    b2 = jnp.stack([unpack_coarse(g2_ref[(first + t) % slots]) for t in range(34)])
    total = lax.fori_loop(
        0, slots, lambda d, sums: sums + g2_ref[d], jnp.zeros((24, 128), F32)
    )
    column = jnp.sum(unpack_coarse(total), axis=0, keepdims=True)
    same = jnp.where(lanes(lambda r, l: r // 32 == l // 32), 1.0, 0.0)
    mean_b2 = dot(jnp.broadcast_to(column, (8, 128)), same)[0:1] * (1.0 / (slots * 1024.0))
    _, _, w2 = level(2)
    q3, _, w3 = level(3)
    factor = (1.0 - w3 * SCREEN) ** 6 * (1.0 - w2 * SCREEN) ** 2 / SCREEN
    lift = mean_b2 * factor
    u2 = start_of(inner(b2), b2[:-2], b2[2:], group_ring, 2)
    r2 = left_of(b2[2:-2], inner(u2), u2[:-2], u2[2:], group_ring, 2)
    pairs = r2.reshape(15, 2, 32, 128)
    pool_ref[...] = (pairs[:, 0] + pairs[:, 1]).reshape(480, 128)
    rows = pool_ref[pl.ds(0, 240, 2), :] + pool_ref[pl.ds(1, 240, 2), :]
    pool = jnp.where(
        lanes(lambda r, l: ((r & 31) // 2 == (l & 15)) & (r // 32 == l // 32)), 0.125, 0.0
    )
    b3 = dot(rows, pool).reshape(15, 16, 128)
    u3 = w3 * b3
    for _ in range(5):
        b3 = inner(b3)
        u3 = sweep_of(b3, inner(u3), u3[:-2], u3[2:], group_ring, 3)
    u3 = (u3 + lift[None]).reshape(80, 128)
    spread = jnp.where(
        lanes(lambda r, l: ((l & 31) // 2 == (r & 31)) & (r // 32 == l // 32)), 1.0, 0.0
    )
    wide = dot(u3, spread)
    pool_ref[pl.ds(0, 80, 2), :] = wide
    pool_ref[pl.ds(1, 80, 2), :] = wide
    lifted = pool_ref[0:160, :].reshape(5, 1, 32, 128)
    u = (u2[11:21].reshape(5, 2, 32, 128) + lifted).reshape(10, 32, 128)
    u = sweep_of(b2[13:21], inner(u), u[:-2], u[2:], group_ring, 2)
    u = sweep_of(b2[14:20], inner(u), u[:-2], u[2:], group_ring, 2)
    final_ref[...] = u
    return jnp.concatenate([final_ref[parity + h] for h in range(5)], axis=0)


def up_kernel(
    me_ref, meta_ref, g2_ref, m2_ref, m1_ref, m0_ref, p1_ref, p2_ref, low_ref, own_ref,
    high_ref, vel_ref, pay_ref,
    pool_ref, final_ref, lift1_ref, b1_ref, u1_ref, v1_ref, lift0_ref, u0_ref, v0_ref,
    ext_ref, stage_ref,
):
    coarse = coarse_part(me_ref[0], g2_ref, pool_ref, final_ref)
    for c in range(3):
        spread = jnp.where(lanes(lambda r, l: r == 32 * c + (l & 63) // 2), 1.0, 0.0)
        wide = dot(coarse, spread)
        lift1_ref[c, pl.ds(0, 160, 2), :] = wide
        lift1_ref[c, pl.ds(1, 160, 2), :] = wide
    spread0 = jnp.where(lanes(lambda r, l: r == l // 2), 1.0, 0.0)

    def b_at(z, c):
        if z < 0:
            return low_ref[z + 3, c]
        return own_ref[z, c] if z < CZ else high_ref[z - CZ, c]

    def component(c, carry):
        for j, ref in enumerate((m2_ref, m1_ref, m0_ref, p1_ref, p2_ref)):
            b1_ref[2 * j], b1_ref[2 * j + 1] = both_layers(ref[c])
        for z in range(-3, 5):
            i = z + 4
            h = z // 2 + 2
            u1_ref[z + 3] = (
                start_of(b1_ref[i], b1_ref[i - 1], b1_ref[i + 1], flat_ring, 1)
                + lift1_ref[c, 64 * h : 64 * h + 64, :]
            )
        for z in range(-2, 4):
            i = z + 3
            v1_ref[z + 2] = sweep_of(
                b1_ref[z + 4], u1_ref[i], u1_ref[i - 1], u1_ref[i + 1], flat_ring, 1
            )
        for z in range(-1, 3):
            i = z + 2
            value = sweep_of(
                b1_ref[z + 4], v1_ref[i], v1_ref[i - 1], v1_ref[i + 1], flat_ring, 1
            )
            wide = dot(value, spread0)
            lift0_ref[z + 1, pl.ds(0, 64, 2), :] = wide
            lift0_ref[z + 1, pl.ds(1, 64, 2), :] = wide
        for z in range(-2, 6):
            u0_ref[z + 2] = (
                start_of(b_at(z, c), b_at(z - 1, c), b_at(z + 1, c), flat_ring, 0)
                + lift0_ref[z // 2 + 1]
            )
        for z in range(-1, 5):
            i = z + 2
            v0_ref[z + 1] = sweep_of(
                b_at(z, c), u0_ref[i], u0_ref[i - 1], u0_ref[i + 1], flat_ring, 0
            )
        for z in range(CZ):
            i = z + 1
            value = sweep_of(
                own_ref[z, c], v0_ref[i], v0_ref[i - 1], v0_ref[i + 1], flat_ring, 0
            )
            vel_ref[z, c] = value
            rounded = value.astype(BF16).astype(F32)
            ext_ref[3 * z + c, 0:128, :] = rounded
            ext_ref[3 * z + c, 128:144, :] = rounded[0:16]
        return carry

    lax.fori_loop(0, 3, component, 0)
    lane = iota((8, 128), 1)
    sub = iota((8, 128), 0)

    def pick(d, carry):
        for order in range(2):

            @pl.when(meta_ref[4 * d + 2 * order] > 0)
            def _():
                base_x = meta_ref[4 * d + 2 * order] - 1
                base_y = meta_ref[4 * d + 2 * order + 1]
                shift = base_x & 7
                row = pl.multiple_of(base_x - shift, 8)
                late = sub >= shift
                for q in range(3):
                    packed = jnp.zeros((8, 128), F32)
                    for g in range(8):
                        v = 8 * q + g
                        start = row + 8 * (v % 2)
                        value = jnp.where(
                            late,
                            ext_ref[v // 2, pl.ds(start, 8), :],
                            ext_ref[v // 2, pl.ds(start + 8, 8), :],
                        )
                        turned = pltpu.roll(value, (BOX * g - base_y) & 127, 1)
                        packed = jnp.where(lane // BOX == g, turned, packed)
                    stage_ref[d, pl.ds(order * ROWS + 8 * q, 8), :] = pltpu.roll(
                        packed, (8 - shift) & 7, 0
                    )

        return carry

    lax.fori_loop(0, pay_ref.shape[0], pick, 0)

    def finish(t, carry):
        pay_ref[t] = stage_ref[t].astype(BF16)
        return carry

    lax.fori_loop(0, pay_ref.shape[0], finish, 0, unroll=4)


def way_up(me, meta, gathered, tiles, low, own, high):
    slots = gathered.shape[0]
    return call(
        up_kernel,
        (
            jax.ShapeDtypeStruct(own.shape, F32),
            jax.ShapeDtypeStruct((slots, 2 * ROWS, 128), BF16),
        ),
        [SMEM, SMEM] + [VMEM] * 9,
        [
            pltpu.VMEM((480, 128), F32),
            pltpu.VMEM((6, 32, 128), F32),
            pltpu.VMEM((3, 320, 128), F32),
            pltpu.VMEM((10, 64, 128), F32),
            pltpu.VMEM((8, 64, 128), F32),
            pltpu.VMEM((6, 64, 128), F32),
            pltpu.VMEM((4, 128, 128), F32),
            pltpu.VMEM((8, 128, 128), F32),
            pltpu.VMEM((6, 128, 128), F32),
            pltpu.VMEM((12, 144, 128), F32),
            pltpu.VMEM((slots, 2 * ROWS, 128), F32),
        ],
        "way_up",
    )(me, meta, gathered, *tiles, low, own, high)


def read_kernel(dest_ref, pay_ref, pos_ref, out_ref, stage_ref, count_ref):
    slots = pay_ref.shape[0]

    def widen(t, carry):
        count_ref[t] = 0
        stage_ref[t] = pay_ref[t].astype(F32)
        return carry

    lax.fori_loop(0, slots, widen, 0, unroll=4)
    lane = iota((8, 128), 1)

    def one(block, carry):
        target = dest_ref[0, block]
        order = count_ref[target]
        count_ref[target] = order + 1
        weight_x, weight_y, weight_z = box_weights(pos_ref, block)
        rows = []
        for q in range(3):
            packed = stage_ref[target, pl.ds(pl.multiple_of(order * ROWS + 8 * q, 8), 8), :]
            turned = [pltpu.roll(packed, (128 - BOX * g) % 128, 1) for g in range(8)]
            for g in range(8):
                rows.append(jnp.where(lane < BOX, turned[g], turned[(g + 7) % 8]))
        left = jnp.concatenate(rows, axis=0)[:, : 2 * BOX].astype(BF16)
        right = jnp.concatenate(split(weight_y), axis=0)
        spread = lax.dot_general(
            left, right, (((1,), (0,)), ((), ())), preferred_element_type=F32
        )
        for c in range(3):
            total = None
            for k in range(CZ):
                kc = 3 * k + c
                part = spread[BOX * kc : BOX * kc + BOX] * weight_z[k : k + 1]
                total = part if total is None else total + part
            out_ref[c, pl.ds(block, 1), :] = jnp.sum(total * weight_x, axis=0, keepdims=True)
        return carry

    lax.fori_loop(0, pos_ref.shape[1], one, 0, unroll=2)


def read(dest, payload, positions):
    slots = payload.shape[0]
    return call(
        read_kernel,
        jax.ShapeDtypeStruct(positions.shape, F32),
        [SMEM, VMEM, VMEM],
        [pltpu.VMEM((slots, 2 * ROWS, 128), F32), pltpu.SMEM((slots,), jnp.int32)],
        "read",
    )(dest, payload, positions)


def moved(value, step):
    size = lax.axis_size(AX)
    return lax.ppermute(value, AX, [(i, (i + step) % size) for i in range(size)])


def exchanged(value):
    return lax.all_to_all(value, AX, split_axis=0, concat_axis=0, tiled=True)


def shards(marker_positions, marker_forces, dest_slab, base_cells, fluid_source):
    slots = lax.axis_size(AX)
    positions = marker_positions.transpose(1, 0, 2)
    forces = marker_forces.transpose(1, 0, 2)
    dest = dest_slab.T
    me = lax.axis_index(AX).astype(jnp.int32).reshape(1)
    payload = exchanged(build(dest, base_cells.T, positions, forces, slots))
    heads = payload[:, 0 : ROWS + 1 : ROWS, 0 : BOX + 1 : BOX]
    meta = heads.astype(jnp.int32).reshape(4 * slots)
    source, bottom, top = place(meta, payload, fluid_source)
    low = moved(top, 1)
    high = moved(bottom, -1)
    tile = fine_down(low, source, high)
    m1, p1 = moved(tile, 1), moved(tile, -1)
    m2, p2 = moved(tile, 2), moved(tile, -2)
    gathered = exchanged(middle_down(m1, tile, p1, slots))
    velocity, picked = way_up(
        me, meta, gathered, (m2, m1, tile, p1, p2), low, source, high
    )
    out = read(dest, exchanged(picked), positions)
    return velocity, out.transpose(1, 0, 2)


def solution(mesh):
    return jax.shard_map(
        shards,
        mesh=mesh,
        in_specs=(P(AX), P(AX), P(AX), P(AX), P(AX)),
        out_specs=(P(AX), P(AX)),
        check_vma=False,
    )
```

time: 698 us -> 248 us (0.36); the launches traced: 687 us -> 246 us
  local copies, waits for them, and re-layouts: 209 us -> 4.8 us
  other arithmetic: 101 us -> 0.05 us
  Pallas kernels: 0 us -> 98.7 us
  matrix products: 98.1 us -> 0 us
  starting transfers between devices: 116 us -> 27.7 us
  waiting for transfers between devices: 102 us -> 36.7 us
  blocking collectives: 43.7 us -> 77 us
  between operations: 15.2 us -> 0.68 us
    pallas_call x0 -> x6, Pallas kernels: none -> 98.7 us  [the longest x1 30.7 us: build(): call(build_kernel, jax.ShapeDtypeStruct((slots, 2 * ROWS, 128), BF16), [S...]
    dot_general x32 -> x0, matrix products: 98.1 us -> none  [the longest x8 33.9 us: pick(): jnp.einsum('gzcxj,gxi->gzcij', along_y, select_x, preferred_element_type=...]
    all_to_all x0 -> x2, blocking collectives: none -> 77 us  [exchanged(): return lax.all_to_all(value, AX, split_axis=0, concat_axis=0, tiled=True)]
    reshape x17 -> x1, local copies, waits for them, and re-layouts: 77.2 us -> 0.78 us  [shards(): meta = heads.astype(jnp.int32).reshape(4 * slots)]
    ppermute x24 -> x6, starting transfers between devices: 82.8 us -> 14.1 us  [moved(): lax.ppermute(value, AX, [(i, (i + step) % size) for i in range(size)])]
    reduce_sum x3 -> x0, local copies, waits for them, and re-layouts: 56.7 us -> none  [restrict(): return jnp.mean(folded, axis=(1, 4, 6))]
    all_to_all x3 -> x1, waiting for transfers between devices: 47.3 us -> 0.01 us  [exchanged(): return lax.all_to_all(value, AX, split_axis=0, concat_axis=0, tiled=True)]
    all_gather x3 -> x0, blocking collectives: 43.7 us -> none  [stacked_from(): pieces = lax.all_gather(pieces, axes[k])]
  transfers between devices with their start and end apart: 28 -> 7, of which waited for: 26 -> 6; matrix products, arithmetic and copies ran while one was open for 9% -> 0% of each run, Pallas kernels for 0% -> 0%
where the time goes in v1:
time: 248 us; the launch traced here: 246 us
  Pallas kernels  98.7 us (40%)
  blocking collectives  77 us (31%)
  waiting for transfers between devices  36.7 us (15%)
  starting transfers between devices  27.7 us (11%)
  local copies, waits for them, and re-layouts  4.8 us (2%)
    all_to_all x2, blocking collectives, exchanged(): return lax.all_to_all(value, AX, split_axis=0, concat_axis=0, tiled=True)  77 us
    ppermute x6, waiting for transfers between devices, moved(): lax.ppermute(value, AX, [(i, (i + step) % size) for i in range(size)])  36.7 us
    pallas_call x1, Pallas kernels, build(): call(build_kernel, jax.ShapeDtypeStruct((slots, 2 * ROWS, 128), BF16), [S...  30.7 us
    pallas_call x1, Pallas kernels, way_up(): call(up_kernel, (jax.ShapeDtypeStruct(own.shape, F32), jax.ShapeDtypeStru...  24.2 us
    pallas_call x1, Pallas kernels, read(): call(read_kernel, jax.ShapeDtypeStruct(positions.shape, F32), [SMEM, VMEM...  21.1 us
    pallas_call x1, Pallas kernels, place(): call(place_kernel, (jax.ShapeDtypeStruct(fluid.shape, F32), jax.ShapeDtyp...  15.3 us
    ppermute x6, starting transfers between devices, moved(): lax.ppermute(value, AX, [(i, (i + step) % size) for i in range(size)])  14.1 us
    all_to_all x1, starting transfers between devices, exchanged(): return lax.all_to_all(value, AX, split_axis=0, concat_axis=0, tiled=True)  13.6 us
  transfers between devices with their start and end apart: 7, of which 6 were waited for; matrix products, arithmetic and copies ran while one was open for 0% of the time, Pallas kernels for 0%

profile of v1, /device:TPU:1, one launch (start us, length us, event | category | flops | bytes accessed | tf_op | source)
XLA Modules:
  0.0 245.5 jit_solution(11880119615568284291)
XLA Ops:
  0.6 30.7 %build.1 = bf16[128,48,128]{2,1,0:T(8,128)(2,1)} custom-call(s32[1,128]{1,0:T(1,128)} %bitcast.10, s32[2,128]{1,0:T(2,128)} %bitcast.12, f32[3,128,256]{2,1,0:T(8,128)} %bitcast.6, f32[3,128,256]{2,1,0:T(8,128)} %bitcast.8), custom_call_target="tpu_custom_call" | custom-call | tf_op jit(solution)/shard_map/build/pallas_call | solution.py:137
  31.3 36.3 %all_to_all.15.pay_ref = bf16[128,48,128]{2,1,0:T(8,128)(2,1)S(1)} all-to-all(bf16[128,48,128]{2,1,0:T(8,128)(2,1)} %build.1), channel_id=1, replica_groups=mesh['gz'=128] {'gz'}, dimensions={0} | all-to-all | bytes 3145728 | tf_op jit(solution)/shard_map/all_to_all | solution.py:595
  67.7 0.0 copy-start
  67.7 1.4 slice.3
  69.1 0.1 reshape.15
  69.1 0.8 reshape.16.meta_ref
  69.9 0.0 copy-done
  69.9 15.3 %place.1 = (f32[4,3,128,128]{3,2,1,0:T(8,128)}, f32[3,3,128,128]{3,2,1,0:T(8,128)}, f32[3,3,128,128]{3,2,1,0:T(8,128)}) custom-call(s32[512]{0:T(512)} %reshape.16.meta_ref, bf16[128,48,128]{2,1,0:T(8,128)(2,1)} %copy-done, f32[4,3,128,128]{3,2,1,0:T(8,128)} %fluid_ref.1), custom_call_target="tpu_custom_call" | custom-call | tf_op jit(solution)/shard_map/place/pallas_call | solution.py:202
  85.2 1.0 collective-permute-start
  86.2 0.0 collective-permute-start.1
  86.2 7.1 %collective-permute-done.low_ref = f32[3,3,128,128]{3,2,1,0:T(8,128)S(1)} collective-permute-done((f32[3,3,128,128]{3,2,1,0:T(8,128)}, f32[3,3,128,128]{3,2,1,0:T(8,128)S(1)}, u32[]{:S(2)}, u32[]{:S(2)}) %collective-permute-start) | collective-permute-done | bytes 589856 | tf_op jit(solution)/shard_map/ppermute | solution.py:591
  93.3 0.0 copy-start.2
  93.3 2.7 %collective-permute-done.1.high_ref = f32[3,3,128,128]{3,2,1,0:T(8,128)S(1)} collective-permute-done((f32[3,3,128,128]{3,2,1,0:T(8,128)}, f32[3,3,128,128]{3,2,1,0:T(8,128)S(1)}, u32[]{:S(2)}, u32[]{:S(2)}) %collective-permute-start.1) | collective-permute-done | bytes 589856 | tf_op jit(solution)/shard_map/ppermute | solution.py:591
  96.0 0.0 copy-start.3
  96.0 0.0 copy-done.2
  96.0 0.8 copy-done.3
  96.8 4.2 %fine_down.1.own_ref.m0_ref = f32[3,64,128]{2,1,0:T(8,128)} custom-call(f32[3,3,128,128]{3,2,1,0:T(8,128)} %copy-done.2, f32[4,3,128,128]{3,2,1,0:T(8,128)} %get-tuple-element.8.own_ref, f32[3,3,128,128]{3,2,1,0:T(8,128)} %copy-done.3), custom_call_target="tpu_custom_call" | custom-call | tf_op jit(solution)/shard_map/fine_down/pallas_call | solution.py:292
  101.1 5.3 %collective-permute-start.3 = (f32[3,64,128]{2,1,0:T(8,128)}, f32[3,64,128]{2,1,0:T(8,128)S(1)}, u32[]{:S(2)}, u32[]{:S(2)}) collective-permute-start(f32[3,64,128]{2,1,0:T(8,128)} %fine_down.1.own_ref.m0_ref), channel_id=1, source_target_pairs={{0,127},{1,0},{2,1},{3,2},{4,3},{5,4},{6,5},{7,6},{8,7},{9,8},{10,... | collective-permute-start | bytes 294920 | tf_op jit(solution)/shard_map/ppermute | solution.py:591
  106.4 0.0 collective-permute-start.2
  106.4 1.2 collective-permute-done.3.high_ref.p1_ref
  107.5 0.0 copy-start.5
  107.5 6.8 %collective-permute-done.2.low_ref.m1_ref = f32[3,64,128]{2,1,0:T(8,128)S(1)} collective-permute-done((f32[3,64,128]{2,1,0:T(8,128)}, f32[3,64,128]{2,1,0:T(8,128)S(1)}, u32[]{:S(2)}, u32[]{:S(2)}) %collective-permute-start.2) | collective-permute-done | bytes 98336 | tf_op jit(solution)/shard_map/ppermute | solution.py:591
  114.4 0.0 copy-done.5
  114.4 0.0 copy-start.6
  114.4 0.6 copy-done.6
  115.0 3.1 %middle_down.1 = f32[128,24,128]{2,1,0:T(8,128)} custom-call(f32[3,64,128]{2,1,0:T(8,128)} %copy-done.6, f32[3,64,128]{2,1,0:T(8,128)} %fine_down.1.own_ref.m0_ref, f32[3,64,128]{2,1,0:T(8,128)} %copy-done.5), custom_call_target="tpu_custom_call" | custom-call | tf_op jit(solution)/shard_map/middle_down/pallas_call | solution.py:353
  118.1 0.0 copy-start.4
  118.1 13.6 %all-to-all-start.1 = ((f32[128,24,128]{2,1,0:T(8,128)}), f32[128,24,128]{2,1,0:T(8,128)S(1)}, u32[]{:S(2)}, u32[]{:S(2)}) async-start(f32[128,24,128]{2,1,0:T(8,128)} %middle_down.1), calls=%async_computation.1 | async-start | bytes 3145728 | tf_op jit(solution)/shard_map/all_to_all | solution.py:595
  131.7 0.0 copy-done.4
  131.7 7.8 %collective-permute-start.5 = (f32[3,64,128]{2,1,0:T(8,128)S(1)}, f32[3,64,128]{2,1,0:T(8,128)S(1)}, u32[]{:S(2)}, u32[]{:S(2)}) collective-permute-start(f32[3,64,128]{2,1,0:T(8,128)S(1)} %copy-done.4), channel_id=1, source_target_pairs={{0,126},{1,127},{2,0},{3,1},{4,2},{5,3},{6,4},{7,5},{8,6},{9,7},{1... | collective-permute-start | bytes 294920 | tf_op jit(solution)/shard_map/ppermute | solution.py:591
  139.5 0.0 collective-permute-start.4
  139.5 12.5 %collective-permute-done.5.p2_ref = f32[3,64,128]{2,1,0:T(8,128)S(1)} collective-permute-done((f32[3,64,128]{2,1,0:T(8,128)S(1)}, f32[3,64,128]{2,1,0:T(8,128)S(1)}, u32[]{:S(2)}, u32[]{:S(2)}) %collective-permute-start.5) | collective-permute-done | bytes 98336 | tf_op jit(solution)/shard_map/ppermute | solution.py:591
  152.0 0.0 copy-start.7
  152.0 6.4 %collective-permute-done.4.m2_ref = f32[3,64,128]{2,1,0:T(8,128)S(1)} collective-permute-done((f32[3,64,128]{2,1,0:T(8,128)S(1)}, f32[3,64,128]{2,1,0:T(8,128)S(1)}, u32[]{:S(2)}, u32[]{:S(2)}) %collective-permute-start.4) | collective-permute-done | bytes 98336 | tf_op jit(solution)/shard_map/ppermute | solution.py:591
  158.4 0.0 copy-start.8
  158.4 0.0 all-to-all-done.1.g2_ref
  158.4 0.0 copy-start.1
  158.4 0.0 copy-done.7
  158.4 0.6 copy-done.8
  159.0 0.5 copy-done.1
  159.6 24.2 %way_up.1 = (f32[4,3,128,128]{3,2,1,0:T(8,128)}, bf16[128,48,128]{2,1,0:T(8,128)(2,1)}) custom-call(s32[1]{0:T(128)} %bitcast.me_ref, s32[512]{0:T(512)} %reshape.16.meta_ref, f32[128,24,128]{2,1,0:T(8,128)} %copy-done.1, f32[3,64,128]{2,1,0:T(8,128)} %copy-done.8, f32[3,64,128]{2,1,0:T(8,128)} %copy-done.6, f32[3,64,128]{2,1,0:T(8,128)} %fine_down.1.own_ref.m0_ref, ...), custom_call_target="tpu_custom_call" | custom-call | tf_op jit(solution)/shard_map/way_up/pallas_call | solution.py:515
  183.8 40.7 %all_to_all.16.pay_ref = bf16[128,48,128]{2,1,0:T(8,128)(2,1)} all-to-all(bf16[128,48,128]{2,1,0:T(8,128)(2,1)} %get-tuple-element.11), channel_id=1, replica_groups=mesh['gz'=128] {'gz'}, dimensions={0} | all-to-all | bytes 3145728 | tf_op jit(solution)/shard_map/all_to_all | solution.py:595
  224.5 21.1 %read.1 = f32[3,128,256]{2,1,0:T(8,128)} custom-call(s32[1,128]{1,0:T(1,128)} %bitcast.11, bf16[128,48,128]{2,1,0:T(8,128)(2,1)} %all_to_all.16.pay_ref, f32[3,128,256]{2,1,0:T(8,128)} %bitcast.7), custom_call_target="tpu_custom_call" | custom-call | tf_op jit(solution)/shard_map/read/pallas_call | solution.py:580
Async XLA Ops:
  67.7 2.2 copy-start
  85.2 8.1 %collective-permute-start = (f32[3,3,128,128]{3,2,1,0:T(8,128)}, f32[3,3,128,128]{3,2,1,0:T(8,128)S(1)}, u32[]{:S(2)}, u32[]{:S(2)}) collective-permute-start(f32[3,3,128,128]{3,2,1,0:T(8,128)} %get-tuple-element.7), channel_id=1, source_target_pairs={{0,1},{1,2},{2,3},{3,4},{4,5},{5,6},{6,7},{7,8},{8,9},{9,10},{10,1... | collective-permute-start | bytes 1769480 | tf_op jit(solution)/shard_map/ppermute | solution.py:591
  86.2 9.8 %collective-permute-start.1 = (f32[3,3,128,128]{3,2,1,0:T(8,128)}, f32[3,3,128,128]{3,2,1,0:T(8,128)S(1)}, u32[]{:S(2)}, u32[]{:S(2)}) collective-permute-start(f32[3,3,128,128]{3,2,1,0:T(8,128)} %get-tuple-element.9), channel_id=1, source_target_pairs={{0,127},{1,0},{2,1},{3,2},{4,3},{5,4},{6,5},{7,6},{8,7},{9,8},{10,... | collective-permute-start | bytes 1769480 | tf_op jit(solution)/shard_map/ppermute | solution.py:591
  93.3 2.7 %copy-start.2 = (f32[3,3,128,128]{3,2,1,0:T(8,128)}, f32[3,3,128,128]{3,2,1,0:T(8,128)S(1)}, u32[]{:S(2)}) copy-start(f32[3,3,128,128]{3,2,1,0:T(8,128)S(1)} %collective-permute-done.low_ref) | copy-start | bytes 1769476
  96.0 0.8 copy-start.3
  101.1 6.5 %collective-permute-start.3 = (f32[3,64,128]{2,1,0:T(8,128)}, f32[3,64,128]{2,1,0:T(8,128)S(1)}, u32[]{:S(2)}, u32[]{:S(2)}) collective-permute-start(f32[3,64,128]{2,1,0:T(8,128)} %fine_down.1.own_ref.m0_ref), channel_id=1, source_target_pairs={{0,127},{1,0},{2,1},{3,2},{4,3},{5,4},{6,5},{7,6},{8,7},{9,8},{10,... | collective-permute-start | bytes 294920 | tf_op jit(solution)/shard_map/ppermute | solution.py:591
  106.4 8.0 %collective-permute-start.2 = (f32[3,64,128]{2,1,0:T(8,128)}, f32[3,64,128]{2,1,0:T(8,128)S(1)}, u32[]{:S(2)}, u32[]{:S(2)}) collective-permute-start(f32[3,64,128]{2,1,0:T(8,128)} %fine_down.1.own_ref.m0_ref), channel_id=1, source_target_pairs={{0,1},{1,2},{2,3},{3,4},{4,5},{5,6},{6,7},{7,8},{8,9},{9,10},{10,1... | collective-permute-start | bytes 294920 | tf_op jit(solution)/shard_map/ppermute | solution.py:591
  107.5 6.8 %copy-start.5 = (f32[3,64,128]{2,1,0:T(8,128)}, f32[3,64,128]{2,1,0:T(8,128)S(1)}, u32[]{:S(2)}) copy-start(f32[3,64,128]{2,1,0:T(8,128)S(1)} %collective-permute-done.3.high_ref.p1_ref) | copy-start | bytes 294916
  114.4 0.6 copy-start.6
  118.1 13.6 %copy-start.4 = (f32[3,64,128]{2,1,0:T(8,128)S(1)}, f32[3,64,128]{2,1,0:T(8,128)}, u32[]{:S(2)}) copy-start(f32[3,64,128]{2,1,0:T(8,128)} %fine_down.1.own_ref.m0_ref) | copy-start | bytes 294916
  118.1 40.3 %all-to-all-start.1 = ((f32[128,24,128]{2,1,0:T(8,128)}), f32[128,24,128]{2,1,0:T(8,128)S(1)}, u32[]{:S(2)}, u32[]{:S(2)}) async-start(f32[128,24,128]{2,1,0:T(8,128)} %middle_down.1), calls=%async_computation.1 | async-start | bytes 3145728 | tf_op jit(solution)/shard_map/all_to_all | solution.py:595
  131.7 20.3 %collective-permute-start.5 = (f32[3,64,128]{2,1,0:T(8,128)S(1)}, f32[3,64,128]{2,1,0:T(8,128)S(1)}, u32[]{:S(2)}, u32[]{:S(2)}) collective-permute-start(f32[3,64,128]{2,1,0:T(8,128)S(1)} %copy-done.4), channel_id=1, source_target_pairs={{0,126},{1,127},{2,0},{3,1},{4,2},{5,3},{6,4},{7,5},{8,6},{9,7},{1... | collective-permute-start | bytes 294920 | tf_op jit(solution)/shard_map/ppermute | solution.py:591
  139.5 18.9 %collective-permute-start.4 = (f32[3,64,128]{2,1,0:T(8,128)S(1)}, f32[3,64,128]{2,1,0:T(8,128)S(1)}, u32[]{:S(2)}, u32[]{:S(2)}) collective-permute-start(f32[3,64,128]{2,1,0:T(8,128)S(1)} %copy-done.4), channel_id=1, source_target_pairs={{0,2},{1,3},{2,4},{3,5},{4,6},{5,7},{6,8},{7,9},{8,10},{9,11},{10,... | collective-permute-start | bytes 294920 | tf_op jit(solution)/shard_map/ppermute | solution.py:591
  152.0 6.4 %copy-start.7 = (f32[3,64,128]{2,1,0:T(8,128)}, f32[3,64,128]{2,1,0:T(8,128)S(1)}, u32[]{:S(2)}) copy-start(f32[3,64,128]{2,1,0:T(8,128)S(1)} %collective-permute-done.5.p2_ref) | copy-start | bytes 294916
  158.4 0.7 copy-start.8
  158.4 1.2 copy-start.1

commit v2 on v1

--- a/solution.py
+++ b/solution.py
@@ -1,3 +1,5 @@
+import math
+
 import jax
 import jax.numpy as jnp
 from jax import lax
@@ -22,20 +24,27 @@
     return q, SCREEN + 6.0 * q, RELAX / (SCREEN + 6.0 * q)
 
 
-def call(body, out_shape, in_specs=None, scratch=(), name=None, out_specs=None):
-    options = {}
-    if in_specs is not None:
-        options["in_specs"] = in_specs
-    if out_specs is not None:
-        options["out_specs"] = out_specs
+def call(body, out_shape, in_specs=None, scratch=(), name=None, megabytes=24):
+    options = {} if in_specs is None else {"in_specs": in_specs}
     return pl.pallas_call(
         body,
         out_shape=out_shape,
         scratch_shapes=list(scratch),
         name=name,
         interpret=INTERPRET,
+        compiler_params=pltpu.CompilerParams(vmem_limit_bytes=megabytes << 20),
         **options,
     )
+
+
+def shaped(shape, dtype, near=True):
+    if near and not INTERPRET:
+        return pltpu.VMEM(shape, dtype)
+    return jax.ShapeDtypeStruct(shape, dtype)
+
+
+def near(value):
+    return value if INTERPRET else pltpu.with_memory_space_constraint(value, pltpu.VMEM)
 
 
 VMEM = pl.BlockSpec(memory_space=pltpu.VMEM)
@@ -47,23 +56,21 @@
 
 
 COS = (
-    0.99999999999999999,
-    -0.30842513753404244,
-    0.015854344243815498,
-    -0.00032599188692738954,
-    3.5908604459003885e-06,
-    -2.4611369504941976e-08,
-    1.1500234922e-10,
+    0.13884009367929634,
+    0.008677498753340366,
+    0.0001925760632832398,
+    2.2059131886721028e-06,
+    1.644977822379996e-08,
 )
 
 
 def phi(offset):
-    square = jnp.minimum(offset * offset, 4.0)
-    value = jnp.full_like(square, COS[-1])
-    for coefficient in COS[-2::-1]:
-        value = value * square + coefficient
-    value = 0.5 * (value * value)
-    return jnp.where(square < 4.0, value, 0.0)
+    inside = jnp.maximum(4.0 - offset * offset, 0.0)
+    value = inside * COS[-1] + COS[-2]
+    for coefficient in COS[-3::-1]:
+        value = value * inside + coefficient
+    value = value * inside
+    return value * value
 
 
 def split(value):
@@ -81,50 +88,63 @@
     return phi(along_x - cells), phi(along_y - cells), phi(height - levels)
 
 
+def by_levels(weight_y, weight_z):
+    return split(jnp.concatenate([weight_z[k : k + 1] * weight_y for k in range(CZ)], axis=0))
+
+
+def together(count, most):
+    return math.gcd(count, most)
+
+
 def build_kernel(dest_ref, base_ref, pos_ref, frc_ref, out_ref, stage_ref, count_ref):
     slots = out_ref.shape[0]
     blocks = pos_ref.shape[1]
+    group = together(blocks, 4)
 
     def clear(t, carry):
         count_ref[t] = 0
-        stage_ref[t] = jnp.zeros((2 * ROWS, 128), F32)
-        return carry
-
-    lax.fori_loop(0, slots, clear, 0)
+        for order in range(2):
+            stage_ref[t, order * ROWS : order * ROWS + 8, :] = jnp.zeros((8, 128), F32)
+        return carry
+
+    lax.fori_loop(0, slots, clear, 0, unroll=4)
     lane = iota((8, 128), 1)
-    sub = iota((8, 128), 0)
-
-    def one(block, carry):
+    top = iota((8, 128), 0) == 0
+
+    def one(block):
         weight_x, weight_y, weight_z = box_weights(pos_ref, block)
-        parts = []
-        loaded = [weight_z * frc_ref[c, pl.ds(block, 1), :] for c in range(3)]
-        for k in range(CZ):
-            for c in range(3):
-                parts.append(loaded[c][k : k + 1, :] * weight_x)
-        whole = jnp.concatenate(parts, axis=0)
-        high, low = split(whole)
-        right = jnp.concatenate(split(weight_y), axis=0)
+        loaded = [frc_ref[c, pl.ds(block, 1), :] * weight_x for c in range(3)]
+        high, low = split(jnp.concatenate(loaded, axis=0))
+        right = jnp.concatenate(by_levels(weight_y, weight_z), axis=0)
         dims = (((1,), (1,)), ((), ()))
-        first = lax.dot_general(high, right, dims, preferred_element_type=F32)
-        second = lax.dot_general(low, right[:BOX], dims, preferred_element_type=F32)
-        box = first[:, :BOX] + first[:, BOX:] + second
-        target = dest_ref[0, block]
-        order = count_ref[target]
-        count_ref[target] = order + 1
+        box = lax.dot_general(high, right, dims, preferred_element_type=F32)
+        box = box + lax.dot_general(low, right, dims, preferred_element_type=F32)
+        box = box + pltpu.roll(box, 64, 1)
         base_x = base_ref[0, block].astype(F32) + 1.0
         base_y = base_ref[1, block].astype(F32)
-        for q in range(3):
-            packed = jnp.concatenate(
-                [box[(8 * q + g) * 8 : (8 * q + g + 1) * 8] for g in range(8)], axis=1
+        tiles = []
+        for c in range(3):
+            tile = jnp.where(
+                lane < 64, box[BOX * c : BOX * c + 8], box[BOX * c + 8 : BOX * c + 16]
             )
-            if q == 0:
-                top = sub == 0
-                packed = jnp.where(top & (lane == 0), base_x, packed)
-                packed = jnp.where(top & (lane == BOX), base_y, packed)
-            stage_ref[target, pl.ds(pl.multiple_of(order * ROWS + 8 * q, 8), 8), :] = packed
-        return carry
-
-    lax.fori_loop(0, blocks, one, 0, unroll=2)
+            if c == 0:
+                tile = jnp.where(top & (lane == 0), base_x, tile)
+                tile = jnp.where(top & (lane == BOX), base_y, tile)
+            tiles.append(tile)
+        return tiles
+
+    def several(step, carry):
+        results = [one(step * group + n) for n in range(group)]
+        for n in range(group):
+            target = dest_ref[0, step * group + n]
+            order = count_ref[target]
+            count_ref[target] = order + 1
+            for c in range(3):
+                row = pl.multiple_of(order * ROWS + 8 * c, 8)
+                stage_ref[target, pl.ds(row, 8), :] = results[n][c]
+        return carry
+
+    lax.fori_loop(0, blocks // group, several, 0)
 
     def finish(t, carry):
         out_ref[t] = stage_ref[t].astype(BF16)
@@ -136,7 +156,7 @@
 def build(dest, base, positions, forces, slots):
     return call(
         build_kernel,
-        jax.ShapeDtypeStruct((slots, 2 * ROWS, 128), BF16),
+        shaped((slots, 2 * ROWS, 128), BF16),
         [SMEM, SMEM, VMEM, VMEM],
         [pltpu.VMEM((slots, 2 * ROWS, 128), F32), pltpu.SMEM((slots,), jnp.int32)],
         "build",
@@ -152,39 +172,53 @@
             grid_ref[3 * z + c, 0:128, :] = fluid_ref[z, c]
             grid_ref[3 * z + c, 128:144, :] = jnp.zeros((16, 128), F32)
 
-    def add(tile, base_x, base_y):
+    def turned(tile, head, base_y):
+        base_x = jnp.maximum(head - 1, 0)
         shift = base_x & 7
         row = pl.multiple_of(base_x - shift, 8)
         window = (lane - base_y) & 127
-        inside = (window >= 1) & (window <= BOX - 2)
+        inside = (window >= 1) & (window <= BOX - 2) & (head > 0)
         late = inside & (sub >= shift)
         early = inside & (sub < shift)
-        rolled = [pltpu.roll(tile[8 * q : 8 * q + 8], shift, 0) for q in range(3)]
-        for kc in range(12):
-            v = 2 * kc
-            first = pltpu.roll(rolled[v // 8], (base_y - BOX * (v % 8)) & 127, 1)
-            second = pltpu.roll(rolled[v // 8], (base_y - BOX * (v % 8 + 1)) & 127, 1)
-            grid_ref[kc, pl.ds(row, 8), :] += jnp.where(late, first, 0.0)
-            grid_ref[kc, pl.ds(row + 8, 8), :] += jnp.where(
-                early, first, jnp.where(late, second, 0.0)
-            )
-            grid_ref[kc, pl.ds(row + 16, 8), :] += jnp.where(early, second, 0.0)
-
-    def source_of(d, carry):
-        for order in range(2):
-
-            @pl.when(meta_ref[4 * d + 2 * order] > 0)
-            def _():
-                tile = pay_ref[d].astype(F32)
-                add(
-                    tile[order * ROWS : (order + 1) * ROWS],
-                    meta_ref[4 * d + 2 * order] - 1,
-                    meta_ref[4 * d + 2 * order + 1],
+        values = []
+        for c in range(3):
+            piece = pltpu.roll(tile[8 * c : 8 * c + 8], shift, 0)
+            for g in range(8):
+                values.append(pltpu.roll(piece, (base_y - BOX * g) & 127, 1))
+        return row, late, early, values
+
+    def add(row, late, early, values):
+        for k in range(CZ):
+            for c in range(3):
+                first = values[8 * c + k]
+                second = values[8 * c + 4 + k]
+                kc = 3 * k + c
+                grid_ref[kc, pl.ds(row, 8), :] += jnp.where(late, first, 0.0)
+                grid_ref[kc, pl.ds(row + 8, 8), :] += jnp.where(
+                    early, first, jnp.where(late, second, 0.0)
                 )
-
-        return carry
-
-    lax.fori_loop(0, slots, source_of, 0)
+                grid_ref[kc, pl.ds(row + 16, 8), :] += jnp.where(early, second, 0.0)
+
+    group = together(slots, 2)
+
+    def several(step, carry):
+        found = []
+        for n in range(group):
+            d = step * group + n
+            tile = pay_ref[d].astype(F32)
+            for order in range(2):
+                found.append(
+                    turned(
+                        tile[order * ROWS : (order + 1) * ROWS],
+                        meta_ref[4 * d + 2 * order],
+                        meta_ref[4 * d + 2 * order + 1],
+                    )
+                )
+        for one in found:
+            add(*one)
+        return carry
+
+    lax.fori_loop(0, slots // group, several, 0)
     for z in range(CZ):
         for c in range(3):
             kc = 3 * z + c
@@ -202,14 +236,14 @@
     return call(
         place_kernel,
         (
-            jax.ShapeDtypeStruct(fluid.shape, F32),
-            jax.ShapeDtypeStruct((3, 3, width, width), F32),
-            jax.ShapeDtypeStruct((3, 3, width, width), F32),
+            shaped(fluid.shape, F32),
+            shaped((3, 3, width, width), F32),
+            shaped((3, 3, width, width), F32),
         ),
         [SMEM, VMEM, VMEM],
         [pltpu.VMEM((12, 144, 128), F32)],
         "place",
-    )(meta, payload, fluid)
+    )(meta, near(payload), fluid)
 
 
 def flat_ring(x):
@@ -291,11 +325,11 @@
 def fine_down(low, own, high):
     return call(
         fine_kernel,
-        jax.ShapeDtypeStruct((3, 64, 128), F32),
+        shaped((3, 64, 128), F32),
         None,
         [pltpu.VMEM((CZ + 2, 128, 128), F32), pltpu.VMEM((128, 128), F32)],
         "fine_down",
-    )(low, own, high)
+    )(near(low), near(own), near(high))
 
 
 def both_layers(tile):
@@ -352,11 +386,11 @@
 def middle_down(low, own, high, slots):
     return call(
         middle_kernel,
-        jax.ShapeDtypeStruct((slots, 24, 128), F32),
+        shaped((slots, 24, 128), F32),
         None,
         [pltpu.VMEM((64, 128), F32)],
         "middle_down",
-    )(low, own, high)
+    )(near(low), near(own), near(high))
 
 
 def inner(x):
@@ -410,7 +444,7 @@
     me_ref, meta_ref, g2_ref, m2_ref, m1_ref, m0_ref, p1_ref, p2_ref, low_ref, own_ref,
     high_ref, vel_ref, pay_ref,
     pool_ref, final_ref, lift1_ref, b1_ref, u1_ref, v1_ref, lift0_ref, u0_ref, v0_ref,
-    ext_ref, stage_ref,
+    ext_ref,
 ):
     coarse = coarse_part(me_ref[0], g2_ref, pool_ref, final_ref)
     for c in range(3):
@@ -473,41 +507,47 @@
     lane = iota((8, 128), 1)
     sub = iota((8, 128), 0)
 
-    def pick(d, carry):
-        for order in range(2):
-
-            @pl.when(meta_ref[4 * d + 2 * order] > 0)
-            def _():
-                base_x = meta_ref[4 * d + 2 * order] - 1
-                base_y = meta_ref[4 * d + 2 * order + 1]
-                shift = base_x & 7
-                row = pl.multiple_of(base_x - shift, 8)
-                late = sub >= shift
-                for q in range(3):
+    half = [lane // BOX == g for g in range(8)]
+
+    def gather(head, base_y):
+        base_x = jnp.maximum(head - 1, 0)
+        shift = base_x & 7
+        row = pl.multiple_of(base_x - shift, 8)
+        late = sub >= shift
+        values = []
+        for k in range(CZ):
+            for c in range(3):
+                tiles = [ext_ref[3 * k + c, pl.ds(row + 8 * n, 8), :] for n in range(3)]
+                for upper in range(2):
+                    value = jnp.where(late, tiles[upper], tiles[upper + 1])
+                    g = 4 * upper + k
+                    values.append((c, g, pltpu.roll(value, (BOX * g - base_y) & 127, 1)))
+        return (8 - shift) & 7, values
+
+    group = together(pay_ref.shape[0], 2)
+
+    def several(step, carry):
+        found = []
+        for n in range(group):
+            d = step * group + n
+            for order in range(2):
+                found.append(
+                    gather(meta_ref[4 * d + 2 * order], meta_ref[4 * d + 2 * order + 1])
+                )
+        for n in range(group):
+            pieces = []
+            for order in range(2):
+                back, values = found[2 * n + order]
+                for c in range(3):
                     packed = jnp.zeros((8, 128), F32)
-                    for g in range(8):
-                        v = 8 * q + g
-                        start = row + 8 * (v % 2)
-                        value = jnp.where(
-                            late,
-                            ext_ref[v // 2, pl.ds(start, 8), :],
-                            ext_ref[v // 2, pl.ds(start + 8, 8), :],
-                        )
-                        turned = pltpu.roll(value, (BOX * g - base_y) & 127, 1)
-                        packed = jnp.where(lane // BOX == g, turned, packed)
-                    stage_ref[d, pl.ds(order * ROWS + 8 * q, 8), :] = pltpu.roll(
-                        packed, (8 - shift) & 7, 0
-                    )
-
-        return carry
-
-    lax.fori_loop(0, pay_ref.shape[0], pick, 0)
-
-    def finish(t, carry):
-        pay_ref[t] = stage_ref[t].astype(BF16)
-        return carry
-
-    lax.fori_loop(0, pay_ref.shape[0], finish, 0, unroll=4)
+                    for own_c, g, value in values:
+                        if own_c == c:
+                            packed = jnp.where(half[g], value, packed)
+                    pieces.append(pltpu.roll(packed, back, 0))
+            pay_ref[step * group + n] = jnp.concatenate(pieces, axis=0).astype(BF16)
+        return carry
+
+    lax.fori_loop(0, pay_ref.shape[0] // group, several, 0)
 
 
 def way_up(me, meta, gathered, tiles, low, own, high):
@@ -515,8 +555,8 @@
     return call(
         up_kernel,
         (
-            jax.ShapeDtypeStruct(own.shape, F32),
-            jax.ShapeDtypeStruct((slots, 2 * ROWS, 128), BF16),
+            shaped(own.shape, F32, False),
+            shaped((slots, 2 * ROWS, 128), BF16),
         ),
         [SMEM, SMEM] + [VMEM] * 9,
         [
@@ -530,10 +570,9 @@
             pltpu.VMEM((8, 128, 128), F32),
             pltpu.VMEM((6, 128, 128), F32),
             pltpu.VMEM((12, 144, 128), F32),
-            pltpu.VMEM((slots, 2 * ROWS, 128), F32),
         ],
         "way_up",
-    )(me, meta, gathered, *tiles, low, own, high)
+    )(me, meta, near(gathered), *map(near, tiles), near(low), near(own), near(high))
 
 
 def read_kernel(dest_ref, pay_ref, pos_ref, out_ref, stage_ref, count_ref):
@@ -547,43 +586,51 @@
     lax.fori_loop(0, slots, widen, 0, unroll=4)
     lane = iota((8, 128), 1)
 
-    def one(block, carry):
-        target = dest_ref[0, block]
-        order = count_ref[target]
-        count_ref[target] = order + 1
+    group = together(pos_ref.shape[1], 4)
+
+    def one(block, target, order):
         weight_x, weight_y, weight_z = box_weights(pos_ref, block)
-        rows = []
-        for q in range(3):
-            packed = stage_ref[target, pl.ds(pl.multiple_of(order * ROWS + 8 * q, 8), 8), :]
-            turned = [pltpu.roll(packed, (128 - BOX * g) % 128, 1) for g in range(8)]
-            for g in range(8):
-                rows.append(jnp.where(lane < BOX, turned[g], turned[(g + 7) % 8]))
-        left = jnp.concatenate(rows, axis=0)[:, : 2 * BOX].astype(BF16)
-        right = jnp.concatenate(split(weight_y), axis=0)
+        lower, upper = [], []
+        for c in range(3):
+            row = pl.multiple_of(order * ROWS + 8 * c, 8)
+            packed = stage_ref[target, pl.ds(row, 8), :]
+            swapped = pltpu.roll(packed, 64, 1)
+            lower.append(jnp.where(lane < 64, packed, swapped))
+            upper.append(jnp.where(lane < 64, swapped, packed))
+        left = jnp.concatenate(
+            [half for pair in zip(lower, upper) for half in pair], axis=0
+        ).astype(BF16)
+        right = jnp.concatenate(by_levels(weight_y, weight_z), axis=0)
         spread = lax.dot_general(
             left, right, (((1,), (0,)), ((), ())), preferred_element_type=F32
         )
         for c in range(3):
-            total = None
-            for k in range(CZ):
-                kc = 3 * k + c
-                part = spread[BOX * kc : BOX * kc + BOX] * weight_z[k : k + 1]
-                total = part if total is None else total + part
-            out_ref[c, pl.ds(block, 1), :] = jnp.sum(total * weight_x, axis=0, keepdims=True)
-        return carry
-
-    lax.fori_loop(0, pos_ref.shape[1], one, 0, unroll=2)
+            value = spread[BOX * c : BOX * c + BOX] * weight_x
+            out_ref[c, pl.ds(block, 1), :] = jnp.sum(value, axis=0, keepdims=True)
+
+    def several(step, carry):
+        places = []
+        for n in range(group):
+            target = dest_ref[0, step * group + n]
+            order = count_ref[target]
+            count_ref[target] = order + 1
+            places.append((target, order))
+        for n in range(group):
+            one(step * group + n, *places[n])
+        return carry
+
+    lax.fori_loop(0, pos_ref.shape[1] // group, several, 0)
 
 
 def read(dest, payload, positions):
     slots = payload.shape[0]
     return call(
         read_kernel,
-        jax.ShapeDtypeStruct(positions.shape, F32),
+        shaped(positions.shape, F32, False),
         [SMEM, VMEM, VMEM],
         [pltpu.VMEM((slots, 2 * ROWS, 128), F32), pltpu.SMEM((slots,), jnp.int32)],
         "read",
-    )(dest, payload, positions)
+    )(dest, near(payload), positions)
 
 
 def moved(value, step):

time: 248 us -> 196 us (0.79)
  Pallas kernels: 98.7 us -> 56.5 us
  blocking collectives: 77 us -> 65 us
  local copies, waits for them, and re-layouts: 4.8 us -> 10.6 us
    pallas_call x6, Pallas kernels: 98.7 us -> 56.5 us  [the longest x1 18.6 us: way_up(): call(up_kernel, (shaped(own.shape, F32, False), shaped((slots, 2 * ROWS,...]
    all_to_all x2, blocking collectives: 77 us -> 65 us  [exchanged(): return lax.all_to_all(value, AX, split_axis=0, concat_axis=0, tiled=True)]
    unnamed x18 -> x26, local copies, waits for them, and re-layouts: 2.65 us -> 9.05 us
where the time goes in v2:
time: 196 us
  blocking collectives  65 us (33%)
  Pallas kernels  56.5 us (29%)
  waiting for transfers between devices  36.6 us (19%)
  starting transfers between devices  26.3 us (13%)
  local copies, waits for them, and re-layouts  10.6 us (5%)
    all_to_all x2, blocking collectives, exchanged(): return lax.all_to_all(value, AX, split_axis=0, concat_axis=0, tiled=True)  65 us
    ppermute x6, waiting for transfers between devices, moved(): lax.ppermute(value, AX, [(i, (i + step) % size) for i in range(size)])  36.6 us
    pallas_call x1, Pallas kernels, way_up(): call(up_kernel, (shaped(own.shape, F32, False), shaped((slots, 2 * ROWS,...  18.6 us
    ppermute x6, starting transfers between devices, moved(): lax.ppermute(value, AX, [(i, (i + step) % size) for i in range(size)])  14.2 us
    pallas_call x1, Pallas kernels, build(): call(build_kernel, shaped((slots, 2 * ROWS, 128), BF16), [SMEM, SMEM, VME...  14 us
    all_to_all x1, starting transfers between devices, exchanged(): return lax.all_to_all(value, AX, split_axis=0, concat_axis=0, tiled=True)  12.1 us
    pallas_call x1, Pallas kernels, place(): call(place_kernel, (shaped(fluid.shape, F32), shaped((3, 3, width, width)...  9.98 us
    pallas_call x1, Pallas kernels, read(): call(read_kernel, shaped(positions.shape, F32, False), [SMEM, VMEM, VMEM]...  9.72 us
  transfers between devices with their start and end apart: 7, of which 6 were waited for; matrix products, arithmetic and copies ran while one was open for 0% of the time, Pallas kernels for 0%

profile of v2, /device:TPU:1, one launch (start us, length us, event | category | flops | bytes accessed | tf_op | source)
XLA Modules:
  0.0 195.7 jit_solution(15053406164894365991)
XLA Ops:
  0.6 0.0 copy-start
  0.6 1.0 copy-done
  1.6 0.0 copy-start.5
  1.6 1.0 copy-done.5
  2.6 0.0 copy-start.10
  2.6 0.7 copy-done.10
  3.3 0.0 copy-start.12
  3.3 0.7 copy-done.12
  4.0 14.0 %build.1 = bf16[128,48,128]{2,1,0:T(8,128)(2,1)S(1)} custom-call(s32[1,128]{1,0:T(1,128)S(1)} %bitcast.9, s32[2,128]{1,0:T(2,128)S(1)} %bitcast.11, f32[3,128,256]{2,1,0:T(8,128)S(1)} %bitcast.6, f32[3,128,256]{2,1,0:T(8,128)S(1)} %bitcast.8), custom_call_target="tpu_custom_call" | custom-call | tf_op jit(solution)/shard_map/build/pallas_call | solution.py:157
  18.0 36.1 %all_to_all.15.pay_ref = bf16[128,48,128]{2,1,0:T(8,128)(2,1)S(1)} all-to-all(bf16[128,48,128]{2,1,0:T(8,128)(2,1)S(1)} %build.1), channel_id=1, replica_groups=mesh['gz'=128] {'gz'}, dimensions={0} | all-to-all | bytes 3145728 | tf_op jit(solution)/shard_map/all_to_all | solution.py:642
  54.1 1.4 slice.3
  55.5 0.1 reshape.15
  55.5 0.2 reshape.16.meta_ref
  55.7 0.0 copy-start.4
  55.7 1.1 copy-done.4
  56.9 10.0 %place.1 = (f32[4,3,128,128]{3,2,1,0:T(8,128)S(1)}, f32[3,3,128,128]{3,2,1,0:T(8,128)S(1)}, f32[3,3,128,128]{3,2,1,0:T(8,128)S(1)}) custom-call(s32[512]{0:T(512)S(1)} %reshape.16.meta_ref, bf16[128,48,128]{2,1,0:T(8,128)(2,1)S(1)} %all_to_all.15.pay_ref, f32[4,3,128,128]{3,2,1,0:T(8,128)S(1)} %copy-done.4), custom_call_target="tpu_custom_call" | custom-call | tf_op jit(solution)/shard_map/place/pallas_call | solution.py:236
  66.9 1.2 collective-permute-start
  68.1 0.0 collective-permute-start.1
  68.1 6.8 %collective-permute-done.low_ref = f32[3,3,128,128]{3,2,1,0:T(8,128)S(1)} collective-permute-done((f32[3,3,128,128]{3,2,1,0:T(8,128)S(1)}, f32[3,3,128,128]{3,2,1,0:T(8,128)S(1)}, u32[]{:S(2)}, u32[]{:S(2)}) %collective-permute-start) | collective-permute-done | bytes 589856 | tf_op jit(solution)/shard_map/ppermute | solution.py:638
  74.9 2.8 %collective-permute-done.1.high_ref = f32[3,3,128,128]{3,2,1,0:T(8,128)S(1)} collective-permute-done((f32[3,3,128,128]{3,2,1,0:T(8,128)S(1)}, f32[3,3,128,128]{3,2,1,0:T(8,128)S(1)}, u32[]{:S(2)}, u32[]{:S(2)}) %collective-permute-start.1) | collective-permute-done | bytes 589856 | tf_op jit(solution)/shard_map/ppermute | solution.py:638
  77.7 2.1 %fine_down.1.own_ref.m0_ref = f32[3,64,128]{2,1,0:T(8,128)S(1)} custom-call(f32[3,3,128,128]{3,2,1,0:T(8,128)S(1)} %collective-permute-done.low_ref, f32[4,3,128,128]{3,2,1,0:T(8,128)S(1)} %get-tuple-element.8.own_ref, f32[3,3,128,128]{3,2,1,0:T(8,128)S(1)} %collective-permute-done.1.high_ref), custom_call_target="tpu_custom_call" | custom-call | tf_op jit(solution)/shard_map/fine_down/pallas_call | solution.py:326
  79.8 5.1 %collective-permute-start.3 = (f32[3,64,128]{2,1,0:T(8,128)S(1)}, f32[3,64,128]{2,1,0:T(8,128)S(1)}, u32[]{:S(2)}, u32[]{:S(2)}) collective-permute-start(f32[3,64,128]{2,1,0:T(8,128)S(1)} %fine_down.1.own_ref.m0_ref), channel_id=1, source_target_pairs={{0,127},{1,0},{2,1},{3,2},{4,3},{5,4},{6,5},{7,6},{8,7},{9,8},{10,... | collective-permute-start | bytes 294920 | tf_op jit(solution)/shard_map/ppermute | solution.py:638
  84.8 0.0 collective-permute-start.2
  84.8 0.9 collective-permute-done.3.high_ref.p1_ref
  85.8 7.0 %collective-permute-done.2.low_ref.m1_ref = f32[3,64,128]{2,1,0:T(8,128)S(1)} collective-permute-done((f32[3,64,128]{2,1,0:T(8,128)S(1)}, f32[3,64,128]{2,1,0:T(8,128)S(1)}, u32[]{:S(2)}, u32[]{:S(2)}) %collective-permute-start.2) | collective-permute-done | bytes 98336 | tf_op jit(solution)/shard_map/ppermute | solution.py:638
  92.8 2.1 %middle_down.1 = f32[128,24,128]{2,1,0:T(8,128)} custom-call(f32[3,64,128]{2,1,0:T(8,128)S(1)} %collective-permute-done.2.low_ref.m1_ref, f32[3,64,128]{2,1,0:T(8,128)S(1)} %fine_down.1.own_ref.m0_ref, f32[3,64,128]{2,1,0:T(8,128)S(1)} %collective-permute-done.3.high_ref.p1_ref), custom_call_target="tpu_custom_call" | custom-call | tf_op jit(solution)/shard_map/middle_down/pallas_call | solution.py:387
  94.9 0.0 copy-start.2
  94.9 0.6 copy-done.2
  95.5 0.0 copy-start.6
  95.5 0.6 copy-done.6
  96.1 0.0 copy-start.8
  96.1 0.6 copy-done.8
  96.8 12.1 %all-to-all-start.1 = ((f32[128,24,128]{2,1,0:T(8,128)}), f32[128,24,128]{2,1,0:T(8,128)S(1)}, u32[]{:S(2)}, u32[]{:S(2)}) async-start(f32[128,24,128]{2,1,0:T(8,128)} %middle_down.1), calls=%async_computation.1 | async-start | bytes 3145728 | tf_op jit(solution)/shard_map/all_to_all | solution.py:642
  108.9 7.9 %collective-permute-start.5 = (f32[3,64,128]{2,1,0:T(8,128)}, f32[3,64,128]{2,1,0:T(8,128)}, u32[]{:S(2)}, u32[]{:S(2)}) collective-permute-start(f32[3,64,128]{2,1,0:T(8,128)} %copy-done.2), channel_id=1, source_target_pairs={{0,126},{1,127},{2,0},{3,1},{4,2},{5,3},{6,4},{7,5},{8,6},{9,7},{1... | collective-permute-start | bytes 294920 | tf_op jit(solution)/shard_map/ppermute | solution.py:638
  116.8 0.0 collective-permute-start.4
  116.8 12.5 %collective-permute-done.5.p2_ref = f32[3,64,128]{2,1,0:T(8,128)} collective-permute-done((f32[3,64,128]{2,1,0:T(8,128)}, f32[3,64,128]{2,1,0:T(8,128)}, u32[]{:S(2)}, u32[]{:S(2)}) %collective-permute-start.5) | collective-permute-done | bytes 98336 | tf_op jit(solution)/shard_map/ppermute | solution.py:638
  129.3 6.5 %collective-permute-done.4.m2_ref = f32[3,64,128]{2,1,0:T(8,128)} collective-permute-done((f32[3,64,128]{2,1,0:T(8,128)}, f32[3,64,128]{2,1,0:T(8,128)}, u32[]{:S(2)}, u32[]{:S(2)}) %collective-permute-start.4) | collective-permute-done | bytes 98336 | tf_op jit(solution)/shard_map/ppermute | solution.py:638
  135.8 0.0 all-to-all-done.1.g2_ref
  135.8 0.0 copy-start.3
  135.8 0.9 copy-done.3
  136.7 0.0 copy-start.7
  136.7 0.9 copy-done.7
  137.6 0.9 copy-done.9
  138.5 18.6 %way_up.1 = (f32[4,3,128,128]{3,2,1,0:T(8,128)}, bf16[128,48,128]{2,1,0:T(8,128)(2,1)S(1)}) custom-call(s32[1]{0:T(128)} %bitcast.me_ref, s32[512]{0:T(512)S(1)} %reshape.16.meta_ref, f32[128,24,128]{2,1,0:T(8,128)S(1)} %all-to-all-done.1.g2_ref, f32[3,64,128]{2,1,0:T(8,128)} %collective-permute-done.4.m2_ref, f32[3,64,128]{2,1,0:T(8,128)S(1)} %copy-done.9, ...), custom_call_target="tpu_custom_call" | custom-call | tf_op jit(solution)/shard_map/way_up/pallas_call | solution.py:555
  157.1 28.9 %all_to_all.16.pay_ref = bf16[128,48,128]{2,1,0:T(8,128)(2,1)S(1)} all-to-all(bf16[128,48,128]{2,1,0:T(8,128)(2,1)S(1)} %get-tuple-element.11), channel_id=1, replica_groups=mesh['gz'=128] {'gz'}, dimensions={0} | all-to-all | bytes 3145728 | tf_op jit(solution)/shard_map/all_to_all | solution.py:642
  186.0 0.0 copy-done.1
  186.0 0.0 copy-done.11
  186.0 9.7 %read.1 = f32[3,128,256]{2,1,0:T(8,128)} custom-call(s32[1,128]{1,0:T(1,128)S(1)} %bitcast.10, bf16[128,48,128]{2,1,0:T(8,128)(2,1)S(1)} %all_to_all.16.pay_ref, f32[3,128,256]{2,1,0:T(8,128)S(1)} %bitcast.7), custom_call_target="tpu_custom_call" | custom-call | tf_op jit(solution)/shard_map/read/pallas_call | solution.py:627
  (3 shorter events, 0.0 us)
Async XLA Ops:
  0.6 1.0 copy-start
  1.6 1.0 copy-start.5
  2.6 0.7 copy-start.10
  3.3 0.7 copy-start.12
  55.7 1.1 copy-start.4
  66.9 8.0 %collective-permute-start = (f32[3,3,128,128]{3,2,1,0:T(8,128)S(1)}, f32[3,3,128,128]{3,2,1,0:T(8,128)S(1)}, u32[]{:S(2)}, u32[]{:S(2)}) collective-permute-start(f32[3,3,128,128]{3,2,1,0:T(8,128)S(1)} %get-tuple-element.7), channel_id=1, source_target_pairs={{0,1},{1,2},{2,3},{3,4},{4,5},{5,6},{6,7},{7,8},{8,9},{9,10},{10,1... | collective-permute-start | bytes 1769480 | tf_op jit(solution)/shard_map/ppermute | solution.py:638
  68.1 9.6 %collective-permute-start.1 = (f32[3,3,128,128]{3,2,1,0:T(8,128)S(1)}, f32[3,3,128,128]{3,2,1,0:T(8,128)S(1)}, u32[]{:S(2)}, u32[]{:S(2)}) collective-permute-start(f32[3,3,128,128]{3,2,1,0:T(8,128)S(1)} %get-tuple-element.9), channel_id=1, source_target_pairs={{0,127},{1,0},{2,1},{3,2},{4,3},{5,4},{6,5},{7,6},{8,7},{9,8},{10,... | collective-permute-start | bytes 1769480 | tf_op jit(solution)/shard_map/ppermute | solution.py:638
  79.8 6.0 %collective-permute-start.3 = (f32[3,64,128]{2,1,0:T(8,128)S(1)}, f32[3,64,128]{2,1,0:T(8,128)S(1)}, u32[]{:S(2)}, u32[]{:S(2)}) collective-permute-start(f32[3,64,128]{2,1,0:T(8,128)S(1)} %fine_down.1.own_ref.m0_ref), channel_id=1, source_target_pairs={{0,127},{1,0},{2,1},{3,2},{4,3},{5,4},{6,5},{7,6},{8,7},{9,8},{10,... | collective-permute-start | bytes 294920 | tf_op jit(solution)/shard_map/ppermute | solution.py:638
  84.8 8.0 %collective-permute-start.2 = (f32[3,64,128]{2,1,0:T(8,128)S(1)}, f32[3,64,128]{2,1,0:T(8,128)S(1)}, u32[]{:S(2)}, u32[]{:S(2)}) collective-permute-start(f32[3,64,128]{2,1,0:T(8,128)S(1)} %fine_down.1.own_ref.m0_ref), channel_id=1, source_target_pairs={{0,1},{1,2},{2,3},{3,4},{4,5},{5,6},{6,7},{7,8},{8,9},{9,10},{10,1... | collective-permute-start | bytes 294920 | tf_op jit(solution)/shard_map/ppermute | solution.py:638
  94.9 0.6 copy-start.2
  95.5 0.6 copy-start.6
  96.1 0.6 copy-start.8
  96.8 39.0 %all-to-all-start.1 = ((f32[128,24,128]{2,1,0:T(8,128)}), f32[128,24,128]{2,1,0:T(8,128)S(1)}, u32[]{:S(2)}, u32[]{:S(2)}) async-start(f32[128,24,128]{2,1,0:T(8,128)} %middle_down.1), calls=%async_computation.1 | async-start | bytes 3145728 | tf_op jit(solution)/shard_map/all_to_all | solution.py:642
  108.9 20.4 %collective-permute-start.5 = (f32[3,64,128]{2,1,0:T(8,128)}, f32[3,64,128]{2,1,0:T(8,128)}, u32[]{:S(2)}, u32[]{:S(2)}) collective-permute-start(f32[3,64,128]{2,1,0:T(8,128)} %copy-done.2), channel_id=1, source_target_pairs={{0,126},{1,127},{2,0},{3,1},{4,2},{5,3},{6,4},{7,5},{8,6},{9,7},{1... | collective-permute-start | bytes 294920 | tf_op jit(solution)/shard_map/ppermute | solution.py:638
  116.8 19.0 %collective-permute-start.4 = (f32[3,64,128]{2,1,0:T(8,128)}, f32[3,64,128]{2,1,0:T(8,128)}, u32[]{:S(2)}, u32[]{:S(2)}) collective-permute-start(f32[3,64,128]{2,1,0:T(8,128)} %copy-done.2), channel_id=1, source_target_pairs={{0,2},{1,3},{2,4},{3,5},{4,6},{5,7},{6,8},{7,9},{8,10},{9,11},{10,... | collective-permute-start | bytes 294920 | tf_op jit(solution)/shard_map/ppermute | solution.py:638
  135.8 0.9 copy-start.3
  136.7 0.9 copy-start.7
  137.6 0.9 copy-start.9
  157.1 28.9 %copy-start.1 = (f32[128,3,256]{2,0,1:T(8,128)S(1)}, f32[128,3,256]{2,0,1:T(8,128)}, u32[]{:S(2)}) copy-start(f32[128,3,256]{2,0,1:T(8,128)} %param.5) | copy-start | bytes 1179652
  157.1 28.9 %copy-start.11 = (s32[128,1]{0,1:T(1,128)S(1)}, s32[128,1]{0,1:T(1,128)}, u32[]{:S(2)}) copy-start(s32[128,1]{0,1:T(1,128)} %param.7) | copy-start | bytes 1540
